TPU v7x, 32 devices: a whole 2x2x4 slice. The times are simulated.
32 devices in a mesh: lat: 4 (over y, x), lon: 4 (over z), mem: 2 (over core).
Axes of the slice: x: 2, y: 2, z: 4, core: 2. Of those that a mesh axis runs over, the one named last changes fastest.
Arguments:
- anomalies: bfloat16 [24, 4, 1440, 512], P('mem', None, 'lon', 'lat'), may hold values from -6 to 6
- taper: float32 [4, 1440, 512], P('lon', 'lat'), may hold values from 0.5 to 8
- obs_row: int32 [256, 512], P('lat', 'lon'), may hold values from 0 to 511, as said below
- obs_col: int32 [256, 512], P('lat', 'lon'), may hold values from 0 to 1439, as said below
- obs_level: int32 [256, 512], P('lat', 'lon'), may hold values from 0 to 3
- obs_value: float32 [256, 512], P('lat', 'lon'), may hold values from -18 to 18
Outputs:
- increment: float32 [4, 1440, 512], P(None, 'lon', 'lat')
Inputs may be any that keep to these rules, and one draw needn't show every extreme that they name: `obs_row`: the entry in row i lies in latitude rows (i // 64) * 128 to (i // 64 + 1) * 128 - 1, drawn evenly there. `obs_col`: the entry in column j lies in longitude columns (j // 128) * 360 to (j // 128 + 1) * 360 - 1, drawn evenly there.
All inputs are finite; a program needn't handle non-finite values.
Results may differ from a plain program's by a relative error of at most 0.0066.
Values may be sent and summed in bfloat16 or wider, within the bound.
A program may use at most 128 MiB of HBM per device.

v0:
```python
import functools
import math

import jax
import jax.numpy as jnp
from jax import lax
from jax.experimental import pallas as pl
from jax.experimental.pallas import tpu as pltpu
from jax.sharding import PartitionSpec as P


def lon_factors(block_count, block_size, part_count, part_size):
    length = block_count * block_size
    nyquist = length // 2
    inner = 24 if block_size % 24 == 0 else next(n for n in range(32, 0, -1) if block_size % n == 0)
    outer = block_size // inner
    coef_idx = jnp.arange(length, dtype=jnp.int32).reshape(part_count, part_size)
    wavenum = jnp.where(coef_idx <= nyquist, coef_idx, coef_idx - nyquist)

    def waves(points, coefs):
        phase_idx = points * coefs % length
        angles = phase_idx.astype(jnp.float32) * (2.0 * math.pi / length)
        return jnp.cos(angles), jnp.sin(angles)

    scales = jnp.where(
        (coef_idx == 0) | (coef_idx == nyquist), 1.0 / math.sqrt(length), math.sqrt(2.0 / length)
    )
    starts = (jnp.arange(block_count, dtype=jnp.int32) * block_size)[:, None, None]
    start_cos, start_sin = waves(starts, wavenum[None])
    is_cos = (coef_idx <= nyquist)[None]
    first = jnp.where(is_cos, start_cos, start_sin) * scales
    second = jnp.where(is_cos, -start_sin, start_cos) * scales
    coarse = jnp.stack([first, second], axis=2)
    high = (jnp.arange(outer, dtype=jnp.int32) * inner)[None, :, None, None]
    low = jnp.arange(inner, dtype=jnp.int32)[None, None, :, None]
    pieces = waves(high, wavenum[:, None, None, :]) + waves(low, wavenum[:, None, None, :])
    high_cos, high_sin, low_cos, low_sin = lax.optimization_barrier(pieces)
    fine = jnp.stack([high_cos * low_cos - high_sin * low_sin, high_sin * low_cos + high_cos * low_sin])
    return coarse, fine.reshape(2, part_count, block_size, part_size)


def lat_basis(length):
    inner = next(size for size in range(32, 0, -1) if length % size == 0)
    outer = length // inner
    mode_idx = jnp.arange(length, dtype=jnp.int32)[None, :]

    def waves(points):
        phase_idx = mode_idx * points[:, None] % (4 * length)
        angles = phase_idx.astype(jnp.float32) * (math.pi / (2.0 * length))
        return jnp.cos(angles), jnp.sin(angles)

    scales = jnp.where(mode_idx == 0, 1.0 / math.sqrt(length), math.sqrt(2.0 / length))
    high_cos, high_sin = waves(jnp.arange(outer, dtype=jnp.int32) * (2 * inner))
    low_cos, low_sin = waves(jnp.arange(inner, dtype=jnp.int32) * 2 + 1)
    high_cos, high_sin, low_cos, low_sin = lax.optimization_barrier(
        (high_cos * scales, high_sin * scales, low_cos, low_sin)
    )
    basis = high_cos[:, None, :] * low_cos[None] - high_sin[:, None, :] * low_sin[None]
    return basis.reshape(length, length).astype(jnp.bfloat16)


def fused_kernel(
    lat_size, lon_size, own, obs_rows,
    anom, taper, level, column, row, value, coarse, fine, modes, out,
    fields, table_fwd, table_inv, fine_near, modes_near, taper_near, taper_all, hits, innov_own, innov_all,
    weighted, inverse, total, partner_part, lat_send, lat_recv, lon_send, lon_recv,
    field_ss, field_rs, local_sem, table_sem, taper_ss, taper_rs, innov_ss, innov_rs,
    gather_ss, gather_rs, mem_sem, lat_ss, lat_rs, lon_ss, lon_rs, pair_sem,
):
    lat, lon, mem = lax.axis_index("lat"), lax.axis_index("lon"), lax.axis_index("mem")
    place_count = lat_size * lon_size
    half = lon_size // 2
    me = lat * lon_size + lon
    col_count, row_count = fields.shape[3:]
    f32, bf16 = jnp.float32, jnp.bfloat16

    def device(lat_idx, lon_idx, mem_idx):
        return {"lat": lat_idx, "lon": lon_idx, "mem": mem_idx}

    def place(offset):
        spot = lax.rem(me + offset, place_count)
        return lax.div(spot, lon_size), lax.rem(spot, lon_size)

    def remote(src, dst, send, recv, target):
        return pltpu.make_async_remote_copy(
            src_ref=src, dst_ref=dst, send_sem=send, recv_sem=recv,
            device_id=target, device_id_type=pl.DeviceIdType.MESH,
        )

    barrier = pltpu.get_barrier_semaphore()

    @pl.loop(1, place_count)
    def _(offset):
        lat_idx, lon_idx = place(offset)
        pl.semaphore_signal(
            barrier, inc=1, device_id=device(lat_idx, lon_idx, mem),
            device_id_type=pl.DeviceIdType.MESH,
        )

    pl.semaphore_signal(
        barrier, inc=1, device_id=device(lat, lon, 1 - mem),
        device_id_type=pl.DeviceIdType.MESH,
    )
    pl.semaphore_wait(barrier, place_count)

    def field_copy(turn, offset):
        lat_idx, lon_idx = place(offset)
        return remote(
            anom.at[lat_idx * own + turn, lon_idx], fields.at[turn, lat, lon],
            field_ss.at[turn, offset], field_rs.at[turn, offset], device(lat_idx, lon_idx, mem),
        )

    def send_fields(turn):
        @pl.loop(1, place_count)
        def _(offset):
            field_copy(turn, offset).start()

    def own_copy(turn):
        return pltpu.make_async_copy(
            anom.at[lat * own + turn, lon], fields.at[turn, lat, lon], local_sem.at[turn]
        )

    send_fields(0)
    taper_copies = [
        remote(
            taper_all.at[lat], taper_all.at[lat], taper_ss.at[step], taper_rs.at[step],
            device(lax.rem(lat + step, lat_size), lon, mem),
        )
        for step in range(1, lat_size)
    ]
    table_copies = [
        pltpu.make_async_copy(src, dst, table_sem.at[idx])
        for idx, (src, dst) in enumerate([
            (taper.at[0], taper_near), (fine, fine_near), (modes, modes_near),
        ])
    ]
    for copy in table_copies:
        copy.start()
    for turn in range(own):
        own_copy(turn).start()

    hits[...] = jnp.zeros_like(hits)
    col_start, row_start = lon * col_count, lat * row_count
    group = 4

    @pl.loop(0, obs_rows // group)
    def _(step):
        def wide(ref):
            return jnp.concatenate([ref[pl.ds(step * group + part, 1), :] for part in range(group)], axis=1)

        keys = wide(level) * col_count + (wide(column) - col_start)
        local_row = wide(row) - row_start
        amount = wide(value)
        width = keys.shape[1]
        high = amount.astype(bf16).astype(f32)
        low = amount - high
        row_hot = lax.broadcasted_iota(jnp.int32, (row_count, width), 0) == local_row
        right = jnp.concatenate(
            [jnp.where(row_hot, high, 0.0).astype(bf16), jnp.where(row_hot, low, 0.0).astype(bf16)], axis=0
        )
        cells = lax.broadcasted_iota(jnp.int32, (col_count, width), 0)
        for lev in range(lon_size):
            left = jnp.where(cells == keys - lev * col_count, 1.0, 0.0).astype(bf16)
            hits[lev] += lax.dot_general(
                left, right, (((1,), (1,)), ((), ())), preferred_element_type=f32
            )

    for lev in range(lon_size):
        innov_own[lev] = (hits[lev, :, :row_count] + hits[lev, :, row_count:]).astype(bf16)
    innov_copies = [
        remote(
            innov_own.at[lax.rem(lon + step, lon_size)], innov_all.at[lat, lon],
            innov_ss.at[step], innov_rs.at[step], device(lat, lax.rem(lon + step, lon_size), mem),
        )
        for step in range(1, lon_size)
    ]
    for copy in innov_copies:
        copy.start()
    innov_local = pltpu.make_async_copy(innov_own.at[lon], innov_all.at[lat, lon], innov_ss.at[0])
    innov_local.start()
    table_copies[0].wait()
    taper_all[lat] = taper_near[...].astype(bf16)
    for copy in taper_copies:
        copy.start()
    send_fields(1)
    for copy in table_copies[1:]:
        copy.wait()

    @pl.loop(0, lon_size)
    def _(block):
        for part in range(lat_size):
            table = (
                coarse[block, part, 0:1, :] * fine_near[0, part]
                + coarse[block, part, 1:2, :] * fine_near[1, part]
            )
            table_inv[block, part] = table.astype(bf16)
            table_fwd[block, part] = table.T.astype(bf16)

    innov_local.wait()
    for copy in innov_copies:
        copy.wait_recv()
    gather_copies = [
        remote(
            innov_all.at[lat], innov_all.at[lat], gather_ss.at[step], gather_rs.at[step],
            device(lax.rem(lat + step, lat_size), lon, mem),
        )
        for step in range(1, lat_size)
    ]
    for copy in gather_copies:
        copy.start()
    for turn in range(2, own):
        send_fields(turn)
    total[...] = jnp.zeros_like(total)
    for copy in taper_copies + gather_copies:
        copy.wait_recv()

    mem_copy = remote(
        total.at[pl.ds((1 - mem) * half, half)], partner_part, mem_sem.at[0], mem_sem.at[1],
        device(lat, lon, 1 - mem),
    )

    @pl.loop(0, own)
    def _(turn):
        def weigh(band, block):
            product = fields[turn, band, block].astype(f32) * innov_all[band, block].astype(f32)
            lanes = pl.ds(pl.multiple_of(band * row_count, row_count), row_count)
            weighted[block, :, lanes] = product.astype(bf16)

        own_copy(turn).wait()
        weigh(lat, lon)

        @pl.loop(1, place_count)
        def _(offset):
            field_copy(turn, offset).wait_recv()
            weigh(*place(place_count - offset))

        @pl.loop(0, lat_size)
        def _(part):
            zonal = jnp.dot(table_fwd[0, part], weighted[0], preferred_element_type=f32)
            for block in range(1, lon_size):
                zonal += jnp.dot(table_fwd[block, part], weighted[block], preferred_element_type=f32)
            spectrum = jnp.dot(zonal.astype(bf16), modes_near[...], preferred_element_type=f32)
            tapered = (spectrum * taper_all[part].astype(f32)).astype(bf16)
            inverse[part] = lax.dot_general(
                tapered, modes_near[...], (((1,), (1,)), ((), ())), preferred_element_type=f32
            ).astype(bf16)

        def localize(step):
            block = lax.rem((1 - mem) * half + step, lon_size)
            localized = jnp.dot(table_inv[block, 0], inverse[0], preferred_element_type=f32)
            for part in range(1, lat_size):
                localized += jnp.dot(table_inv[block, part], inverse[part], preferred_element_type=f32)
            for band in range(lat_size):
                total[block, band] += (
                    fields[turn, band, block].astype(f32)
                    * localized[:, band * row_count:(band + 1) * row_count]
                )

        pl.loop(0, half)(localize)
        pl.when(turn == own - 1)(lambda: mem_copy.start())
        pl.loop(half, lon_size)(localize)

    mem_copy.wait_recv()
    lat_copies = [
        [
            remote(
                lat_send.at[block, lax.rem(lat + step, lat_size)], lat_recv.at[block, step],
                lat_ss.at[block, step], lat_rs.at[block, step],
                device(lax.rem(lat + step, lat_size), lon, mem),
            )
            for step in range(1, lat_size)
        ]
        for block in range(half)
    ]
    for block in range(half):
        for band in range(lat_size):
            lat_send[block, band] = (total[mem * half + block, band] + partner_part[block, band]).astype(bf16)
        for copy in lat_copies[block]:
            copy.start()

    def lon_copy(block):
        return remote(
            lon_send.at[block], lon_recv.at[lon], lon_ss.at[block], lon_rs.at[lon],
            device(lat, mem * half + block, mem),
        )

    def lon_local(block):
        return pltpu.make_async_copy(lon_send.at[block], lon_recv.at[lon], lon_ss.at[block])

    for block in range(half):
        for copy in lat_copies[block]:
            copy.wait_recv()
        summed = lat_send[block, lat].astype(f32)
        for step in range(1, lat_size):
            summed += lat_recv[block, step].astype(f32)
        lon_send[block] = summed.astype(bf16)
        pl.when(mem * half + block != lon)(lambda block=block: lon_copy(block).start())
        pl.when(mem * half + block == lon)(lambda block=block: lon_local(block).start())
    receives = lax.div(lon, half) == mem
    pair_copy = remote(lon_recv, lon_recv, pair_sem.at[0], pair_sem.at[1], device(lat, lon, 1 - mem))

    @pl.when(receives)
    def _():
        for step in range(1, lon_size):
            sender = lax.rem(lon + step, lon_size)
            remote(
                lon_send.at[0], lon_recv.at[sender], lon_ss.at[0], lon_rs.at[sender],
                device(lat, sender, mem),
            ).wait_recv()

    for block in range(half):
        pl.when(mem * half + block != lon)(lambda block=block: lon_copy(block).wait_send())
        pl.when(mem * half + block == lon)(lambda block=block: lon_local(block).wait())

    @pl.when(receives)
    def _():
        pair_copy.start()
        pair_copy.wait_send()

    @pl.when(jnp.logical_not(receives))
    def _():
        pair_copy.wait_recv()

    out[...] = lon_recv[...]
    mem_copy.wait_send()
    for copy in taper_copies + innov_copies + gather_copies + sum(lat_copies, []):
        copy.wait_send()

    @pl.loop(0, own)
    def _(turn):
        @pl.loop(1, place_count)
        def _(offset):
            field_copy(turn, offset).wait_send()


def local(anomalies, taper, obs_row, obs_col, obs_level, obs_value):
    member_count, level_count, col_count, row_count = anomalies.shape
    lon_size, lat_size = lax.axis_size("lon"), lax.axis_size("lat")
    lon_total, lat_total = col_count * lon_size, row_count * lat_size
    ensemble = member_count * lax.axis_size("mem")
    own = member_count // lat_size
    place_count = lat_size * lon_size
    half = lon_size // 2
    part_count = taper.shape[1]
    coarse, fine = lon_factors(lon_size, col_count, lat_size, part_count)
    lat_table = lat_basis(lat_total)
    f32, bf16 = jnp.float32, jnp.bfloat16
    slab = (col_count, row_count)
    whole = pl.BlockSpec(memory_space=pl.ANY)
    near = pl.BlockSpec(memory_space=pltpu.VMEM)
    dma = pltpu.SemaphoreType.DMA
    result = pl.pallas_call(
        functools.partial(fused_kernel, lat_size, lon_size, own, obs_row.shape[0]),
        out_shape=jax.ShapeDtypeStruct((level_count,) + slab, bf16),
        in_specs=[whole, whole, near, near, near, near, near, whole, whole],
        out_specs=near,
        scratch_shapes=[
            pltpu.VMEM((own, lat_size, lon_size) + slab, bf16),
            pltpu.VMEM((lon_size, lat_size, part_count, col_count), bf16),
            pltpu.VMEM((lon_size, lat_size, col_count, part_count), bf16),
            pltpu.VMEM((2, lat_size, col_count, part_count), f32),
            pltpu.VMEM((lat_total, lat_total), bf16),
            pltpu.VMEM((part_count, lat_total), f32),
            pltpu.VMEM((lat_size, part_count, lat_total), bf16),
            pltpu.VMEM((level_count, col_count, 2 * row_count), f32),
            pltpu.VMEM((level_count,) + slab, bf16),
            pltpu.VMEM((lat_size, lon_size) + slab, bf16),
            pltpu.VMEM((lon_size, col_count, lat_total), bf16),
            pltpu.VMEM((lat_size, part_count, lat_total), bf16),
            pltpu.VMEM((lon_size, lat_size) + slab, f32),
            pltpu.VMEM((half, lat_size) + slab, f32),
            pltpu.VMEM((half, lat_size) + slab, bf16),
            pltpu.VMEM((half, lat_size) + slab, bf16),
            pltpu.VMEM((half,) + slab, bf16),
            pltpu.VMEM((level_count,) + slab, bf16),
            dma((own, place_count)), dma((own, place_count)), dma((own,)), dma((3,)),
            dma((lat_size,)), dma((lat_size,)), dma((lon_size,)), dma((lon_size,)),
            dma((lat_size,)), dma((lat_size,)), dma((2,)), dma((half, lat_size)), dma((half, lat_size)),
            dma((half,)), dma((lon_size,)), dma((2,)),
        ],
        compiler_params=pltpu.CompilerParams(
            collective_id=0, has_side_effects=True, vmem_limit_bytes=60 * 1024 * 1024
        ),
    )(
        anomalies, taper, obs_level, obs_col, obs_row, obs_value, coarse, fine, lat_table,
    )
    return result.astype(f32) / (ensemble - 1)


def solution(mesh):
    in_specs = (
        P("mem", None, "lon", "lat"),
        P("lon", "lat", None),
        P("lat", "lon"),
        P("lat", "lon"),
        P("lat", "lon"),
        P("lat", "lon"),
    )
    out_specs = P(None, "lon", "lat")
    return jax.shard_map(local, mesh=mesh, in_specs=in_specs, out_specs=out_specs, check_vma=False)
```

profile of v0, /device:TPU:0, one launch (start us, length us, event | category | flops | bytes accessed | tf_op | source)
XLA Modules:
  0.0 151.1 jit_solution(9094909221047684432)
XLA Ops:
  0.0 0.6 fusion.4
  0.6 0.5 fusion.11
  1.1 0.5 multiply_subtract_fusion
  1.7 2.3 %pad_maximum_fusion.fine = f32[2,4,360,360]{3,2,1,0:T(8,128)} fusion(f32[1,4,360,360]{3,2,1,0:T(8,128)S(1)} %bitcast.8, f32[1,4,360,360]{3,2,1,0:T(8,128)S(1)} %bitcast.7), kind=kLoop, calls=%fused_computation | loop fusion | flops 1036800 | bytes 8294400 | tf_op jit(solution)/shard_map/stack | solution.py:38
  4.0 0.3 fusion.23
  4.3 0.2 sine_multiply_fusion
  4.6 1.0 subtract_convert_fusion
  5.5 0.9 fusion.28
  6.5 0.7 pad_maximum_fusion.1.coarse
  7.1 142.0 %shard_map.64 = bf16[4,360,128]{2,1,0:T(8,128)(2,1)} custom-call(bf16[12,4,360,128]{3,2,1,0:T(8,128)(2,1)} %anom.1, f32[1,360,512]{2,1,0:T(8,128)} %taper.1, s32[64,128]{1,0:T(8,128)} %level.1, s32[64,128]{1,0:T(8,128)} %column.1, s32[64,128]{1,0:T(8,128)} %row.1, f32[64,128]{1,0:T(8,128)} %value.1, f32[4,4,2,360]{3,2,1,0:T(2,128)} %pad_maximum_fusion.1.coarse, ...), custom_call_target="tpu_custom_call" | custom-call | tf_op jit(solution)/shard_map/pallas_call | solution.py:352
  149.2 1.9 %convert_multiply_fusion = f32[4,360,128]{2,1,0:T(8,128)} fusion(bf16[4,360,128]{2,1,0:T(8,128)(2,1)} %shard_map.64), kind=kLoop, calls=%fused_computation.4 | loop fusion | flops 368640 | bytes 1105920 | tf_op jit(solution)/shard_map/div | solution.py:387
  (8 shorter events, 0.0 us)
where the time goes:
time: 152 us; the launch traced here: 151 us
  Pallas kernels  142 us (93%)
  other arithmetic  8.99 us (6%)
    pallas_call x1, Pallas kernels, local(): pl.pallas_call(functools.partial(fused_kernel, lat_size, lon_size, own, o...  142 us

commit v1 on v0

v1 whole, which is shorter than its diff:
```python
import functools
import math

import jax
import jax.numpy as jnp
import numpy as np
from jax import lax
from jax.experimental import pallas as pl
from jax.experimental.pallas import tpu as pltpu
from jax.sharding import PartitionSpec as P


def lon_seeds(block_count, block_size, part_count, part_size):
    length = block_count * block_size
    nyquist = length // 2
    inner = 24 if block_size % 24 == 0 else next(n for n in range(32, 0, -1) if block_size % n == 0)
    outer = block_size // inner
    coef_idx = np.arange(length).reshape(part_count, part_size)
    wavenum = np.where(coef_idx <= nyquist, coef_idx, coef_idx - nyquist)

    def waves(points):
        angles = (points[None, :, None] * wavenum[:, None, :] % length) * (2.0 * math.pi / length)
        return np.cos(angles), np.sin(angles)

    scales = np.where((coef_idx == 0) | (coef_idx == nyquist), 1.0 / math.sqrt(length), math.sqrt(2.0 / length))
    start_cos, start_sin = waves(np.arange(block_count) * block_size)
    is_cos = (coef_idx <= nyquist)[:, None, :]
    first = np.where(is_cos, start_cos, start_sin) * scales[:, None, :]
    second = np.where(is_cos, -start_sin, start_cos) * scales[:, None, :]
    coarse = np.stack([first, second], axis=2).transpose(1, 0, 2, 3)
    high = np.stack(waves(np.arange(outer) * inner))
    low = np.stack(waves(np.arange(inner)))
    return [jnp.asarray(part, jnp.float32) for part in (coarse, high, low)]


def lat_seeds(length):
    inner = next(size for size in range(32, 0, -1) if length % size == 0)
    outer = length // inner
    mode_idx = np.arange(length)[None, :]

    def waves(points):
        angles = (mode_idx * points[:, None] % (4 * length)) * (math.pi / (2.0 * length))
        return np.cos(angles), np.sin(angles)

    scales = np.where(mode_idx == 0, 1.0 / math.sqrt(length), math.sqrt(2.0 / length))
    high = np.stack(waves(np.arange(outer) * (2 * inner))) * scales
    low = np.stack(waves(np.arange(inner) * 2 + 1))
    return [jnp.asarray(part, jnp.float32) for part in (high, low)]


def fused_kernel(
    lat_size, lon_size, own, obs_rows,
    anom, taper, level, column, row, value, coarse, lon_high, lon_low, lat_high, lat_low, out,
    fields, table_fwd, table_inv, fine, modes, taper_near, taper_all, hits, innov_own, innov_all,
    weighted, spectrum, inverse, total, partner_part, lat_send, lat_recv, lon_send, lon_recv,
    level_near, column_near, row_near, value_near, coarse_near, high_near, low_near, lat_high_near, lat_low_near,
    field_ss, field_rs, local_sem, table_sem, taper_ss, taper_rs, innov_ss, innov_rs,
    gather_ss, gather_rs, share_ss, share_rs, mem_ss, mem_rs, lat_ss, lat_rs, lon_ss, lon_rs, pair_ss, pair_rs,
):
    lat, lon, mem = lax.axis_index("lat"), lax.axis_index("lon"), lax.axis_index("mem")
    place_count = lat_size * lon_size
    half = lon_size // 2
    quarter = half // 2
    me = lat * lon_size + lon
    side = lax.div(lon, half)
    receives = lax.div(lax.rem(lon, half), quarter) == mem
    col_count, row_count = fields.shape[3:]
    f32, bf16 = jnp.float32, jnp.bfloat16

    def device(lat_idx, lon_idx, mem_idx):
        return {"lat": lat_idx, "lon": lon_idx, "mem": mem_idx}

    partner = device(lat, lon, 1 - mem)

    def remote(src, dst, send, recv, target):
        return pltpu.make_async_remote_copy(
            src_ref=src, dst_ref=dst, send_sem=send, recv_sem=recv,
            device_id=target, device_id_type=pl.DeviceIdType.MESH,
        )

    def owned(idx, core):
        near = lax.div(idx, quarter)
        return (1 - side + near * (2 * side - 1)) * half + core * quarter + lax.rem(idx, quarter)

    barrier = pltpu.get_barrier_semaphore()

    @pl.loop(1, place_count)
    def _(offset):
        spot = lax.rem(me + offset, place_count)
        pl.semaphore_signal(
            barrier, inc=1, device_id=device(lax.div(spot, lon_size), lax.rem(spot, lon_size), mem),
            device_id_type=pl.DeviceIdType.MESH,
        )

    pl.semaphore_signal(barrier, inc=1, device_id=partner, device_id_type=pl.DeviceIdType.MESH)
    pl.semaphore_wait(barrier, place_count)

    def field_copy(turn, slot, step):
        lat_idx, lon_idx = lax.rem(lat + slot, lat_size), lax.rem(lon + step, lon_size)
        return remote(
            anom.at[lat_idx * own + turn, lon_idx], fields.at[turn, slot, lon],
            field_ss.at[turn, slot, step], field_rs.at[turn, slot, step], device(lat_idx, lon_idx, mem),
        )

    def send_fields(turn, slot):
        @pl.loop(1 if slot == 0 else 0, lon_size)
        def _(step):
            field_copy(turn, slot, step).start()

    def own_copy(turn):
        return pltpu.make_async_copy(
            anom.at[lat * own + turn, lon], fields.at[turn, 0, lon], local_sem.at[turn]
        )

    lead = lat_size // 2
    for slot in range(lead):
        send_fields(0, slot)
    near_copies = [
        pltpu.make_async_copy(src, dst, table_sem.at[idx])
        for idx, (src, dst) in enumerate([
            (level, level_near), (column, column_near), (row, row_near), (value, value_near),
            (taper.at[0], taper_near), (coarse, coarse_near), (lon_high, high_near), (lon_low, low_near),
            (lat_high, lat_high_near), (lat_low, lat_low_near),
        ])
    ]
    for copy in near_copies:
        copy.start()
    for turn in range(own):
        own_copy(turn).start()

    hits[...] = jnp.zeros_like(hits)
    col_start, row_start = lon * col_count, lat * row_count
    group = 4
    for copy in near_copies[:4]:
        copy.wait()

    @pl.loop(0, obs_rows // group)
    def _(step):
        def wide(ref):
            return jnp.concatenate([ref[pl.ds(step * group + part, 1), :] for part in range(group)], axis=1)

        keys = wide(level_near) * col_count + (wide(column_near) - col_start)
        local_row = wide(row_near) - row_start
        amount = wide(value_near)
        width = keys.shape[1]
        high = amount.astype(bf16).astype(f32)
        low = amount - high
        row_hot = lax.broadcasted_iota(jnp.int32, (row_count, width), 0) == local_row
        right = jnp.concatenate(
            [jnp.where(row_hot, high, 0.0).astype(bf16), jnp.where(row_hot, low, 0.0).astype(bf16)], axis=0
        )
        cells = lax.broadcasted_iota(jnp.int32, (col_count, width), 0)
        for idx in range(half):
            left = jnp.where(cells == keys - owned(idx, mem) * col_count, 1.0, 0.0).astype(bf16)
            hits[idx] += lax.dot_general(
                left, right, (((1,), (1,)), ((), ())), preferred_element_type=f32
            )

    def innov_copy(idx):
        lev = owned(idx, mem)
        return remote(
            innov_own.at[idx], innov_all.at[0, lon], innov_ss.at[idx], innov_rs.at[lon], device(lat, lev, mem)
        )

    for idx in range(half):
        block = (hits[idx, :, :row_count] + hits[idx, :, row_count:]).astype(bf16)
        innov_own[idx] = block
        lev = owned(idx, mem)
        pl.when(lev != lon)(lambda idx=idx: innov_copy(idx).start())

        @pl.when(lev == lon)
        def _(block=block):
            innov_all[0, lon] = block

    for slot in range(lead, lat_size):
        send_fields(0, slot)
    near_copies[4].wait()
    taper_all[lat] = taper_near[...].astype(bf16)
    taper_copies = [
        remote(
            taper_all.at[lat], taper_all.at[lat], taper_ss.at[step], taper_rs.at[step],
            device(lax.rem(lat + step, lat_size), lon, mem),
        )
        for step in range(1, lat_size)
    ]
    for copy in taper_copies:
        copy.start()
    for copy in near_copies[5:]:
        copy.wait()

    outer, inner = high_near.shape[2], low_near.shape[2]

    @pl.loop(0, lat_size)
    def _(part):
        low_cos, low_sin = low_near[0, part], low_near[1, part]
        for idx in range(outer):
            high_cos, high_sin = high_near[0, part, idx:idx + 1, :], high_near[1, part, idx:idx + 1, :]
            rows = slice(idx * inner, (idx + 1) * inner)
            fine[0, rows, :] = high_cos * low_cos - high_sin * low_sin
            fine[1, rows, :] = high_sin * low_cos + high_cos * low_sin

        @pl.loop(0, lon_size)
        def _(block):
            table = (
                coarse_near[block, part, 0:1, :] * fine[0] + coarse_near[block, part, 1:2, :] * fine[1]
            )
            table_inv[block, part] = table.astype(bf16)
            table_fwd[block, part] = table.T.astype(bf16)

    lat_inner = lat_low_near.shape[1]
    per_band = row_count // lat_inner
    lat_cos, lat_sin = lat_low_near[0], lat_low_near[1]
    for slot in range(lat_size):
        band = lax.rem(lat + lat_size - slot, lat_size)
        for idx in range(per_band):
            spot = pl.ds(band * per_band + idx, 1)
            rows = slice(slot * row_count + idx * lat_inner, slot * row_count + (idx + 1) * lat_inner)
            modes[rows, :] = (
                lat_high_near[0, spot, :] * lat_cos - lat_high_near[1, spot, :] * lat_sin
            ).astype(bf16)

    def gather_copy(slot):
        return remote(
            innov_all.at[0], innov_all.at[slot], gather_ss.at[slot], gather_rs.at[slot],
            device(lax.rem(lat + slot, lat_size), lon, mem),
        )

    def share_copy(slot):
        return remote(innov_all.at[slot], innov_all.at[slot], share_ss.at[slot], share_rs.at[slot], partner)

    @pl.when(receives)
    def _():
        for step in range(1, lon_size):
            sender = lax.rem(lon + step, lon_size)
            remote(
                innov_own.at[0], innov_all.at[0, sender], innov_ss.at[0], innov_rs.at[sender],
                device(lat, sender, mem),
            ).wait_recv()
        for slot in range(1, lat_size):
            gather_copy(slot).start()
        share_copy(0).start()

    for turn in range(1, own):
        for slot in range(lat_size):
            send_fields(turn, slot)

    @pl.when(receives)
    def _():
        for slot in range(1, lat_size):
            gather_copy(slot).wait_recv()
            share_copy(slot).start()

    @pl.when(jnp.logical_not(receives))
    def _():
        for slot in range(lat_size):
            share_copy(slot).wait_recv()

    total[...] = jnp.zeros_like(total)
    for copy in taper_copies:
        copy.wait_recv()

    def transform(turn):
        def weigh(slot, block, lanes):
            weighted[block, :, lanes] = fields[turn, slot, block] * innov_all[slot, block]

        for stage in range(lat_size // 2):
            for which in range(2):
                slot = 2 * stage + which
                lanes = slice(which * row_count, (which + 1) * row_count)
                if slot == 0:
                    own_copy(turn).wait()
                    weigh(0, lon, lanes)

                @pl.loop(1 if slot == 0 else 0, lon_size)
                def _(step, slot=slot, lanes=lanes):
                    field_copy(turn, slot, step).wait_recv()
                    weigh(slot, lax.rem(lon + lon_size - step, lon_size), lanes)

            rows = slice(2 * stage * row_count, 2 * (stage + 1) * row_count)

            @pl.loop(0, lat_size)
            def _(part, stage=stage, rows=rows):
                zonal = jnp.dot(table_fwd[0, part], weighted[0], preferred_element_type=f32)
                for block in range(1, lon_size):
                    zonal += jnp.dot(table_fwd[block, part], weighted[block], preferred_element_type=f32)
                terms = jnp.dot(zonal.astype(bf16), modes[rows, :], preferred_element_type=f32)
                if stage > 0:
                    terms += spectrum[part]
                if stage < lat_size // 2 - 1:
                    spectrum[part] = terms
                else:
                    tapered = (terms * taper_all[part].astype(f32)).astype(bf16)
                    inverse[part] = lax.dot_general(
                        tapered, modes[...], (((1,), (1,)), ((), ())), preferred_element_type=f32
                    ).astype(bf16)

    def localize(turn, block):
        localized = jnp.dot(table_inv[block, 0], inverse[0], preferred_element_type=f32)
        for part in range(1, lat_size):
            localized += jnp.dot(table_inv[block, part], inverse[part], preferred_element_type=f32)
        for slot in range(lat_size):
            total[block, slot] += (
                fields[turn, slot, block].astype(f32)
                * localized[:, slot * row_count:(slot + 1) * row_count]
            )

    @pl.loop(0, own - 1)
    def _(turn):
        transform(turn)
        pl.loop(0, lon_size)(lambda block: localize(turn, block))

    transform(own - 1)

    def mem_copy(idx):
        return remote(
            total.at[owned(idx, 1 - mem)], partner_part.at[idx], mem_ss.at[idx], mem_rs.at[idx], partner
        )

    @pl.loop(0, half)
    def _(idx):
        localize(own - 1, owned(idx, 1 - mem))
        mem_copy(idx).start()

    def lat_copy(idx, slot):
        return remote(
            lat_send.at[idx, slot], lat_recv.at[idx, slot], lat_ss.at[idx, slot], lat_rs.at[idx, slot],
            device(lax.rem(lat + lat_size - slot, lat_size), lon, mem),
        )

    @pl.loop(0, half)
    def _(idx):
        block = owned(idx, mem)
        localize(own - 1, block)
        mem_copy(idx).wait_recv()
        for slot in list(range(1, lat_size)) + [0]:
            lat_send[idx, slot] = (total[block, slot] + partner_part[idx, slot]).astype(bf16)
            if slot > 0:
                lat_copy(idx, slot).start()

    def lon_copy(idx):
        return remote(
            lon_send.at[idx], lon_recv.at[lon], lon_ss.at[idx], lon_rs.at[lon], device(lat, owned(idx, mem), mem)
        )

    for idx in range(half):
        summed = lat_send[idx, 0].astype(f32)
        for slot in range(1, lat_size):
            lat_copy(idx, slot).wait_recv()
            summed += lat_recv[idx, slot].astype(f32)
        block = owned(idx, mem)
        lon_send[idx] = summed.astype(bf16)
        pl.when(block != lon)(lambda idx=idx: lon_copy(idx).start())

        @pl.when(block == lon)
        def _(idx=idx):
            lon_recv[lon] = lon_send[idx]

    def pair_copy(sender):
        return remote(lon_recv.at[sender], lon_recv.at[sender], pair_ss.at[sender], pair_rs.at[sender], partner)

    far = [(1 - side) * half + idx for idx in range(half)]
    close = [side * half + lax.rem(lon + idx, half) for idx in range(1, half)]

    @pl.when(receives)
    def _():
        pair_copy(lon).start()
        for sender in far + close:
            remote(
                lon_send.at[0], lon_recv.at[sender], lon_ss.at[0], lon_rs.at[sender], device(lat, sender, mem)
            ).wait_recv()
            pair_copy(sender).start()

    @pl.when(jnp.logical_not(receives))
    def _():
        for sender in far + close + [lon]:
            pair_copy(sender).wait_recv()

    out[...] = lon_recv[...]

    @pl.when(receives)
    def _():
        for sender in far + close + [lon]:
            pair_copy(sender).wait_send()
        for slot in range(1, lat_size):
            gather_copy(slot).wait_send()
        for slot in range(lat_size):
            share_copy(slot).wait_send()

    for idx in range(half):
        pl.when(owned(idx, mem) != lon)(lambda idx=idx: lon_copy(idx).wait_send())
        pl.when(owned(idx, mem) != lon)(lambda idx=idx: innov_copy(idx).wait_send())
        mem_copy(idx).wait_send()
        for slot in range(1, lat_size):
            lat_copy(idx, slot).wait_send()
    for copy in taper_copies:
        copy.wait_send()

    @pl.loop(0, own)
    def _(turn):
        for slot in range(lat_size):
            @pl.loop(1 if slot == 0 else 0, lon_size)
            def _(step, slot=slot):
                field_copy(turn, slot, step).wait_send()


def local(anomalies, taper, obs_row, obs_col, obs_level, obs_value):
    member_count, level_count, col_count, row_count = anomalies.shape
    lon_size, lat_size = lax.axis_size("lon"), lax.axis_size("lat")
    lat_total = row_count * lat_size
    ensemble = member_count * lax.axis_size("mem")
    own = member_count // lat_size
    half = lon_size // 2
    part_count = taper.shape[1]
    seeds = lon_seeds(lon_size, col_count, lat_size, part_count) + lat_seeds(lat_total)
    f32, bf16 = jnp.float32, jnp.bfloat16
    slab = (col_count, row_count)
    whole = pl.BlockSpec(memory_space=pl.ANY)
    dma = pltpu.SemaphoreType.DMA
    obs = [(table.shape, table.dtype) for table in (obs_level, obs_col, obs_row, obs_value)]
    near = obs + [(seed.shape, f32) for seed in seeds]
    result = pl.pallas_call(
        functools.partial(fused_kernel, lat_size, lon_size, own, obs_row.shape[0]),
        out_shape=jax.ShapeDtypeStruct((level_count,) + slab, bf16),
        in_specs=[whole] * 11,
        out_specs=pl.BlockSpec(memory_space=pltpu.VMEM),
        scratch_shapes=[
            pltpu.VMEM((own, lat_size, lon_size) + slab, bf16),
            pltpu.VMEM((lon_size, lat_size, part_count, col_count), bf16),
            pltpu.VMEM((lon_size, lat_size, col_count, part_count), bf16),
            pltpu.VMEM((2, col_count, part_count), f32),
            pltpu.VMEM((lat_total, lat_total), bf16),
            pltpu.VMEM((part_count, lat_total), f32),
            pltpu.VMEM((lat_size, part_count, lat_total), bf16),
            pltpu.VMEM((half, col_count, 2 * row_count), f32),
            pltpu.VMEM((half,) + slab, bf16),
            pltpu.VMEM((lat_size, lon_size) + slab, bf16),
            pltpu.VMEM((lon_size, col_count, 2 * row_count), bf16),
            pltpu.VMEM((lat_size, part_count, lat_total), f32),
            pltpu.VMEM((lat_size, part_count, lat_total), bf16),
            pltpu.VMEM((lon_size, lat_size) + slab, f32),
            pltpu.VMEM((half, lat_size) + slab, f32),
            pltpu.VMEM((half, lat_size) + slab, bf16),
            pltpu.VMEM((half, lat_size) + slab, bf16),
            pltpu.VMEM((half,) + slab, bf16),
            pltpu.VMEM((level_count,) + slab, bf16),
            *[pltpu.VMEM(shape, dtype) for shape, dtype in near],
            dma((own, lat_size, lon_size)), dma((own, lat_size, lon_size)), dma((own,)), dma((10,)),
            dma((lat_size,)), dma((lat_size,)), dma((half,)), dma((lon_size,)),
            dma((lat_size,)), dma((lat_size,)), dma((lat_size,)), dma((lat_size,)),
            dma((half,)), dma((half,)), dma((half, lat_size)), dma((half, lat_size)),
            dma((half,)), dma((lon_size,)), dma((lon_size,)), dma((lon_size,)),
        ],
        compiler_params=pltpu.CompilerParams(
            collective_id=0, has_side_effects=True, vmem_limit_bytes=60 * 1024 * 1024
        ),
    )(
        anomalies, taper, obs_level, obs_col, obs_row, obs_value, *seeds,
    )
    return result.astype(f32) / (ensemble - 1)


def solution(mesh):
    in_specs = (
        P("mem", None, "lon", "lat"),
        P("lon", "lat", None),
        P("lat", "lon"),
        P("lat", "lon"),
        P("lat", "lon"),
        P("lat", "lon"),
    )
    out_specs = P(None, "lon", "lat")
    return jax.shard_map(local, mesh=mesh, in_specs=in_specs, out_specs=out_specs, check_vma=False)
```

time: 152 us -> 137 us (0.901)
  Pallas kernels: 142 us -> 134 us
  other arithmetic: 8.99 us -> 1.91 us
    pallas_call x1, Pallas kernels: 142 us -> 134 us  [local(): pl.pallas_call(functools.partial(fused_kernel, lat_size, lon_size, own, o...]
    another operation x2 -> x0, other arithmetic: 2.98 us -> none  [the longest x1 2.31 us: lon_factors(): jnp.stack([high_cos * low_cos - high_sin * low_sin, high_sin * low_cos +...]
where the time goes in v1:
time: 137 us; the launch traced here: 136 us
  Pallas kernels  134 us (98%)
  other arithmetic  1.91 us (1%)
    pallas_call x1, Pallas kernels, local(): pl.pallas_call(functools.partial(fused_kernel, lat_size, lon_size, own, o...  134 us

profile of v1, /device:TPU:0, one launch (start us, length us, event | category | flops | bytes accessed | tf_op | source)
XLA Modules:
  0.0 136.4 jit_solution(6461693641536003841)
XLA Ops:
  0.0 134.5 %shard_map.109 = bf16[4,360,128]{2,1,0:T(8,128)(2,1)} custom-call(bf16[12,4,360,128]{3,2,1,0:T(8,128)(2,1)} %anom.1, f32[1,360,512]{2,1,0:T(8,128)} %taper.1, s32[64,128]{1,0:T(8,128)} %level.1, s32[64,128]{1,0:T(8,128)} %column.1, s32[64,128]{1,0:T(8,128)} %row.1, f32[64,128]{1,0:T(8,128)} %value.1, f32[4,4,2,360]{3,2,1,0:T(2,128)} %constant.13.clone.coarse, ...), custom_call_target="tpu_custom_call" | custom-call | tf_op jit(solution)/shard_map/pallas_call | solution.py:421
  134.5 1.9 %convert_multiply_fusion = f32[4,360,128]{2,1,0:T(8,128)} fusion(bf16[4,360,128]{2,1,0:T(8,128)(2,1)} %shard_map.109), kind=kLoop, calls=%fused_computation | loop fusion | flops 368640 | bytes 1105920 | tf_op jit(solution)/shard_map/div | solution.py:459

commit v2 on v1

--- a/solution.py
+++ b/solution.py
@@ -10,27 +10,43 @@
 from jax.sharding import PartitionSpec as P
 
 
-def lon_seeds(block_count, block_size, part_count, part_size):
-    length = block_count * block_size
+CLASSES = (0, 2, 1, 3)
+
+
+def round_up(size, unit):
+    return -(-size // unit) * unit
+
+
+def lon_seeds(length, part_count):
     nyquist = length // 2
-    inner = 24 if block_size % 24 == 0 else next(n for n in range(32, 0, -1) if block_size % n == 0)
-    outer = block_size // inner
-    coef_idx = np.arange(length).reshape(part_count, part_size)
+    quarter = length // 4
+    inner = next(n for n in range(24, 0, -8) if quarter % n == 0)
+    outer = quarter // inner
+    share = quarter // part_count
+    padded = round_up(share, 16)
+    offsets = np.arange(padded)
+    coef_idx = np.stack([
+        np.stack([part * (length // part_count) + 4 * offsets + kind for part in range(part_count)])
+        for kind in CLASSES
+    ])
+    real = np.broadcast_to(offsets < share, coef_idx.shape).reshape(-1)
+    coef_idx = np.where(real, coef_idx.reshape(-1), 0)
     wavenum = np.where(coef_idx <= nyquist, coef_idx, coef_idx - nyquist)
 
     def waves(points):
-        angles = (points[None, :, None] * wavenum[:, None, :] % length) * (2.0 * math.pi / length)
+        angles = (points[:, None] * wavenum[None, :] % length) * (2.0 * math.pi / length)
         return np.cos(angles), np.sin(angles)
 
     scales = np.where((coef_idx == 0) | (coef_idx == nyquist), 1.0 / math.sqrt(length), math.sqrt(2.0 / length))
-    start_cos, start_sin = waves(np.arange(block_count) * block_size)
-    is_cos = (coef_idx <= nyquist)[:, None, :]
-    first = np.where(is_cos, start_cos, start_sin) * scales[:, None, :]
-    second = np.where(is_cos, -start_sin, start_cos) * scales[:, None, :]
-    coarse = np.stack([first, second], axis=2).transpose(1, 0, 2, 3)
-    high = np.stack(waves(np.arange(outer) * inner))
+    scales = np.where(real, scales, 0.0)
+    is_cos = coef_idx <= nyquist
+    starts = np.arange(2)[:, None] * quarter + np.arange(outer)[None, :] * inner
+    high_cos, high_sin = waves(starts.reshape(-1))
+    first = np.where(is_cos, high_cos, high_sin) * scales
+    second = np.where(is_cos, -high_sin, high_cos) * scales
+    high = np.stack([first, second]).reshape(2, 2, outer, -1)
     low = np.stack(waves(np.arange(inner)))
-    return [jnp.asarray(part, jnp.float32) for part in (coarse, high, low)]
+    return [jnp.asarray(part, jnp.float32) for part in (high, low)]
 
 
 def lat_seeds(length):
@@ -50,11 +66,11 @@
 
 def fused_kernel(
     lat_size, lon_size, own, obs_rows,
-    anom, taper, level, column, row, value, coarse, lon_high, lon_low, lat_high, lat_low, out,
-    fields, table_fwd, table_inv, fine, modes, taper_near, taper_all, hits, innov_own, innov_all,
-    weighted, spectrum, inverse, total, partner_part, lat_send, lat_recv, lon_send, lon_recv,
-    level_near, column_near, row_near, value_near, coarse_near, high_near, low_near, lat_high_near, lat_low_near,
-    field_ss, field_rs, local_sem, table_sem, taper_ss, taper_rs, innov_ss, innov_rs,
+    anom, taper, level, column, row, value, lon_high, lon_low, lat_high, lat_low, out,
+    fields, even_fwd, odd_fwd, even_inv, odd_inv, fine, modes, taper_near, taper_all, hits, innov_own, innov_all,
+    folded, zonal, spectrum, tapered, inverse, total, partner_part, lat_send, lat_recv, lon_send, lon_recv,
+    level_near, column_near, row_near, value_near, high_near, low_near, lat_high_near, lat_low_near,
+    field_ss, field_rs, local_sem, table_sem, taper_ss, taper_rs, trade_ss, trade_rs, innov_ss, innov_rs,
     gather_ss, gather_rs, share_ss, share_rs, mem_ss, mem_rs, lat_ss, lat_rs, lon_ss, lon_rs, pair_ss, pair_rs,
 ):
     lat, lon, mem = lax.axis_index("lat"), lax.axis_index("lon"), lax.axis_index("mem")
@@ -119,7 +135,7 @@
         pltpu.make_async_copy(src, dst, table_sem.at[idx])
         for idx, (src, dst) in enumerate([
             (level, level_near), (column, column_near), (row, row_near), (value, value_near),
-            (taper.at[0], taper_near), (coarse, coarse_near), (lon_high, high_near), (lon_low, low_near),
+            (taper.at[0], taper_near), (lon_high, high_near), (lon_low, low_near),
             (lat_high, lat_high_near), (lat_low, lat_low_near),
         ])
     ]
@@ -175,37 +191,60 @@
     for slot in range(lead, lat_size):
         send_fields(0, slot)
     near_copies[4].wait()
-    taper_all[lat] = taper_near[...].astype(bf16)
-    taper_copies = [
-        remote(
-            taper_all.at[lat], taper_all.at[lat], taper_ss.at[step], taper_rs.at[step],
-            device(lax.rem(lat + step, lat_size), lon, mem),
-        )
-        for step in range(1, lat_size)
-    ]
-    for copy in taper_copies:
-        copy.start()
+    share, share_pad = taper_near.shape[0] // 4, taper_all.shape[2]
+    modes_half = taper_near.shape[1] // 2
+    spread = (4 * share_pad, 4 * share)
+    out_row = lax.broadcasted_iota(jnp.int32, spread, 0)
+    in_row = lax.broadcasted_iota(jnp.int32, spread, 1)
+    chosen = jnp.zeros(spread, jnp.bool_)
+    for idx, kind in enumerate(CLASSES):
+        local_row = out_row - idx * share_pad
+        chosen |= (local_row >= 0) & (local_row < share) & (in_row == 4 * local_row + kind)
+    by_class = jnp.dot(
+        jnp.where(chosen, 1.0, 0.0).astype(bf16), taper_near[...].astype(bf16), preferred_element_type=f32
+    ).astype(bf16)
+    for idx in range(4):
+        taper_all[idx, lat] = by_class[idx * share_pad:(idx + 1) * share_pad]
+    lanes = pl.ds(pl.multiple_of(mem * modes_half, modes_half), modes_half)
+
+    def taper_copy(step):
+        part = taper_all.at[:, lat, :, lanes]
+        return remote(
+            part, part, taper_ss.at[step], taper_rs.at[step], device(lax.rem(lat + step, lat_size), lon, mem)
+        )
+
+    def trade_copy(step):
+        part = taper_all.at[:, lax.rem(lat + lat_size - step, lat_size), :, lanes]
+        return remote(part, part, trade_ss.at[step], trade_rs.at[step], partner)
+
+    for step in range(1, lat_size):
+        taper_copy(step).start()
     for copy in near_copies[5:]:
         copy.wait()
 
-    outer, inner = high_near.shape[2], low_near.shape[2]
-
-    @pl.loop(0, lat_size)
-    def _(part):
-        low_cos, low_sin = low_near[0, part], low_near[1, part]
+    outer, inner = high_near.shape[2], low_near.shape[1]
+    points, kind_size = even_inv.shape[1:]
+    span = outer * inner
+    low_cos, low_sin = low_near[0], low_near[1]
+    fine[span:, :] = jnp.zeros((points - span, 4 * kind_size), f32)
+    for block in range(2):
+        first = 2 * block * kind_size
         for idx in range(outer):
-            high_cos, high_sin = high_near[0, part, idx:idx + 1, :], high_near[1, part, idx:idx + 1, :]
-            rows = slice(idx * inner, (idx + 1) * inner)
-            fine[0, rows, :] = high_cos * low_cos - high_sin * low_sin
-            fine[1, rows, :] = high_sin * low_cos + high_cos * low_sin
-
-        @pl.loop(0, lon_size)
-        def _(block):
-            table = (
-                coarse_near[block, part, 0:1, :] * fine[0] + coarse_near[block, part, 1:2, :] * fine[1]
+            fine[idx * inner:(idx + 1) * inner, first:] = (
+                high_near[0, block, idx:idx + 1, first:] * low_cos[:, first:]
+                + high_near[1, block, idx:idx + 1, first:] * low_sin[:, first:]
             )
-            table_inv[block, part] = table.astype(bf16)
-            table_fwd[block, part] = table.T.astype(bf16)
+        for kind in range(2 * block, 4):
+            tile = fine[:, kind * kind_size:(kind + 1) * kind_size]
+            if kind < 2:
+                even_inv[kind] = tile.astype(bf16)
+                even_fwd[kind] = tile.T.astype(bf16)
+            else:
+                rows = slice(block * points, (block + 1) * points)
+                cols = slice((kind - 2) * kind_size, (kind - 1) * kind_size)
+                odd_inv[rows, cols] = tile.astype(bf16)
+                odd_fwd[cols, rows] = tile.T.astype(bf16)
+    folded[...] = jnp.zeros_like(folded)
 
     lat_inner = lat_low_near.shape[1]
     per_band = row_count // lat_inner
@@ -256,70 +295,109 @@
             share_copy(slot).wait_recv()
 
     total[...] = jnp.zeros_like(total)
-    for copy in taper_copies:
-        copy.wait_recv()
+    for step in range(1, lat_size):
+        taper_copy(step).wait_recv()
+        trade_copy(step).start()
+    for step in range(1, lat_size):
+        trade_copy(step).wait_recv()
+
+    stages = lat_size // 2
+    pair = 2 * row_count
+    fourth = lon_size // 4
+    kinds = 4 * kind_size
+
+    def fold(turn, slot, lanes):
+        def quarter_of(which):
+            parts = []
+            for idx in range(fourth):
+                block = which * fourth + idx
+                parts.append(fields[turn, slot, block].astype(f32) * innov_all[slot, block].astype(f32))
+            return parts[0] if fourth == 1 else jnp.concatenate(parts, axis=0)
+
+        first, second, third, last = [quarter_of(which) for which in range(4)]
+        even, odd = first + third, second + last
+        for idx, value in enumerate([even + odd, even - odd, first - third, second - last]):
+            folded[pl.ds(idx * points, span), lanes] = value.astype(bf16)
 
     def transform(turn):
-        def weigh(slot, block, lanes):
-            weighted[block, :, lanes] = fields[turn, slot, block] * innov_all[slot, block]
-
-        for stage in range(lat_size // 2):
+        @pl.loop(0, stages)
+        def _(stage):
             for which in range(2):
                 slot = 2 * stage + which
-                lanes = slice(which * row_count, (which + 1) * row_count)
-                if slot == 0:
-                    own_copy(turn).wait()
-                    weigh(0, lon, lanes)
-
-                @pl.loop(1 if slot == 0 else 0, lon_size)
-                def _(step, slot=slot, lanes=lanes):
-                    field_copy(turn, slot, step).wait_recv()
-                    weigh(slot, lax.rem(lon + lon_size - step, lon_size), lanes)
-
-            rows = slice(2 * stage * row_count, 2 * (stage + 1) * row_count)
-
-            @pl.loop(0, lat_size)
-            def _(part, stage=stage, rows=rows):
-                zonal = jnp.dot(table_fwd[0, part], weighted[0], preferred_element_type=f32)
-                for block in range(1, lon_size):
-                    zonal += jnp.dot(table_fwd[block, part], weighted[block], preferred_element_type=f32)
-                terms = jnp.dot(zonal.astype(bf16), modes[rows, :], preferred_element_type=f32)
-                if stage > 0:
-                    terms += spectrum[part]
-                if stage < lat_size // 2 - 1:
-                    spectrum[part] = terms
-                else:
-                    tapered = (terms * taper_all[part].astype(f32)).astype(bf16)
-                    inverse[part] = lax.dot_general(
-                        tapered, modes[...], (((1,), (1,)), ((), ())), preferred_element_type=f32
-                    ).astype(bf16)
-
-    def localize(turn, block):
-        localized = jnp.dot(table_inv[block, 0], inverse[0], preferred_element_type=f32)
-        for part in range(1, lat_size):
-            localized += jnp.dot(table_inv[block, part], inverse[part], preferred_element_type=f32)
-        for slot in range(lat_size):
-            total[block, slot] += (
-                fields[turn, slot, block].astype(f32)
-                * localized[:, slot * row_count:(slot + 1) * row_count]
+
+                @pl.loop(0, lon_size)
+                def _(step, slot=slot):
+                    pl.when(slot + step == 0)(lambda: own_copy(turn).wait())
+                    pl.when(slot + step > 0)(lambda: field_copy(turn, slot, step).wait_recv())
+
+                fold(turn, slot, slice(which * row_count, (which + 1) * row_count))
+            for kind in range(2):
+                zonal[kind * kind_size:(kind + 1) * kind_size, :] = jnp.dot(
+                    even_fwd[kind], folded[kind * points:(kind + 1) * points, :], preferred_element_type=f32
+                ).astype(bf16)
+            zonal[2 * kind_size:, :] = jnp.dot(
+                odd_fwd[...], folded[2 * points:, :], preferred_element_type=f32
+            ).astype(bf16)
+            terms = jnp.dot(
+                zonal[...], modes[pl.ds(pl.multiple_of(stage * pair, pair), pair), :], preferred_element_type=f32
             )
+
+            @pl.when(stage == 0)
+            def _():
+                spectrum[...] = terms
+
+            @pl.when(stage > 0)
+            def _():
+                spectrum[...] += terms
+
+        tapered[...] = (
+            spectrum[...] * taper_all[...].reshape(kinds, lat_size * row_count).astype(f32)
+        ).astype(bf16)
+        inverse[...] = lax.dot_general(
+            tapered[...], modes[...], (((1,), (1,)), ((), ())), preferred_element_type=f32
+        ).astype(bf16)
+
+    def localize(turn, stage):
+        lanes = pl.ds(pl.multiple_of(stage * pair, pair), pair)
+
+        def back(table, rows):
+            return jnp.dot(table, inverse[rows, lanes], preferred_element_type=f32)
+
+        even = back(even_inv[0, :span], slice(0, kind_size))
+        swing = back(even_inv[1, :span], slice(kind_size, 2 * kind_size))
+        odd = [back(odd_inv[idx * points:idx * points + span, :], slice(2 * kind_size, kinds)) for idx in range(2)]
+        for which in range(4):
+            base = even + swing if which % 2 == 0 else even - swing
+            values = base + odd[which % 2] if which < 2 else base - odd[which % 2]
+            for idx in range(fourth):
+                block = which * fourth + idx
+                for part in range(2):
+                    slot = 2 * stage + part
+                    total[block, slot] += (
+                        fields[turn, slot, block].astype(f32)
+                        * values[idx * col_count:(idx + 1) * col_count, part * row_count:(part + 1) * row_count]
+                    )
 
     @pl.loop(0, own - 1)
     def _(turn):
         transform(turn)
-        pl.loop(0, lon_size)(lambda block: localize(turn, block))
+        pl.loop(0, stages)(lambda stage: localize(turn, stage))
 
     transform(own - 1)
 
-    def mem_copy(idx):
-        return remote(
-            total.at[owned(idx, 1 - mem)], partner_part.at[idx], mem_ss.at[idx], mem_rs.at[idx], partner
-        )
-
-    @pl.loop(0, half)
-    def _(idx):
-        localize(own - 1, owned(idx, 1 - mem))
-        mem_copy(idx).start()
+    def mem_copy(idx, stage):
+        slots = pl.ds(2 * stage, 2)
+        return remote(
+            total.at[owned(idx, 1 - mem), slots], partner_part.at[idx, slots],
+            mem_ss.at[idx, stage], mem_rs.at[idx, stage], partner,
+        )
+
+    @pl.loop(0, stages)
+    def _(step):
+        stage = stages - 1 - step
+        localize(own - 1, stage)
+        for idx in range(half):
+            mem_copy(idx, stage).start()
 
     def lat_copy(idx, slot):
         return remote(
@@ -330,12 +408,12 @@
     @pl.loop(0, half)
     def _(idx):
         block = owned(idx, mem)
-        localize(own - 1, block)
-        mem_copy(idx).wait_recv()
-        for slot in list(range(1, lat_size)) + [0]:
-            lat_send[idx, slot] = (total[block, slot] + partner_part[idx, slot]).astype(bf16)
-            if slot > 0:
-                lat_copy(idx, slot).start()
+        for stage in range(stages - 1, -1, -1):
+            mem_copy(idx, stage).wait_recv()
+            for slot in (2 * stage + 1, 2 * stage):
+                lat_send[idx, slot] = (total[block, slot] + partner_part[idx, slot]).astype(bf16)
+                if slot > 0:
+                    lat_copy(idx, slot).start()
 
     def lon_copy(idx):
         return remote(
@@ -389,11 +467,13 @@
     for idx in range(half):
         pl.when(owned(idx, mem) != lon)(lambda idx=idx: lon_copy(idx).wait_send())
         pl.when(owned(idx, mem) != lon)(lambda idx=idx: innov_copy(idx).wait_send())
-        mem_copy(idx).wait_send()
+        for stage in range(stages):
+            mem_copy(idx, stage).wait_send()
         for slot in range(1, lat_size):
             lat_copy(idx, slot).wait_send()
-    for copy in taper_copies:
-        copy.wait_send()
+    for step in range(1, lat_size):
+        taper_copy(step).wait_send()
+        trade_copy(step).wait_send()
 
     @pl.loop(0, own)
     def _(turn):
@@ -411,7 +491,10 @@
     own = member_count // lat_size
     half = lon_size // 2
     part_count = taper.shape[1]
-    seeds = lon_seeds(lon_size, col_count, lat_size, part_count) + lat_seeds(lat_total)
+    lon_total = col_count * lon_size
+    seeds = lon_seeds(lon_total, lat_size) + lat_seeds(lat_total)
+    share_pad = round_up(part_count // 4, 16)
+    kind_size, points = lat_size * share_pad, round_up(lon_total // 4, 128)
     f32, bf16 = jnp.float32, jnp.bfloat16
     slab = (col_count, row_count)
     whole = pl.BlockSpec(memory_space=pl.ANY)
@@ -421,22 +504,26 @@
     result = pl.pallas_call(
         functools.partial(fused_kernel, lat_size, lon_size, own, obs_row.shape[0]),
         out_shape=jax.ShapeDtypeStruct((level_count,) + slab, bf16),
-        in_specs=[whole] * 11,
+        in_specs=[whole] * 10,
         out_specs=pl.BlockSpec(memory_space=pltpu.VMEM),
         scratch_shapes=[
             pltpu.VMEM((own, lat_size, lon_size) + slab, bf16),
-            pltpu.VMEM((lon_size, lat_size, part_count, col_count), bf16),
-            pltpu.VMEM((lon_size, lat_size, col_count, part_count), bf16),
-            pltpu.VMEM((2, col_count, part_count), f32),
+            pltpu.VMEM((2, kind_size, points), bf16),
+            pltpu.VMEM((2 * kind_size, 2 * points), bf16),
+            pltpu.VMEM((2, points, kind_size), bf16),
+            pltpu.VMEM((2 * points, 2 * kind_size), bf16),
+            pltpu.VMEM((points, 4 * kind_size), f32),
             pltpu.VMEM((lat_total, lat_total), bf16),
             pltpu.VMEM((part_count, lat_total), f32),
-            pltpu.VMEM((lat_size, part_count, lat_total), bf16),
+            pltpu.VMEM((4, lat_size, share_pad, lat_total), bf16),
             pltpu.VMEM((half, col_count, 2 * row_count), f32),
             pltpu.VMEM((half,) + slab, bf16),
             pltpu.VMEM((lat_size, lon_size) + slab, bf16),
-            pltpu.VMEM((lon_size, col_count, 2 * row_count), bf16),
-            pltpu.VMEM((lat_size, part_count, lat_total), f32),
-            pltpu.VMEM((lat_size, part_count, lat_total), bf16),
+            pltpu.VMEM((4 * points, 2 * row_count), bf16),
+            pltpu.VMEM((4 * kind_size, 2 * row_count), bf16),
+            pltpu.VMEM((4 * kind_size, lat_total), f32),
+            pltpu.VMEM((4 * kind_size, lat_total), bf16),
+            pltpu.VMEM((4 * kind_size, lat_total), bf16),
             pltpu.VMEM((lon_size, lat_size) + slab, f32),
             pltpu.VMEM((half, lat_size) + slab, f32),
             pltpu.VMEM((half, lat_size) + slab, bf16),
@@ -444,10 +531,10 @@
             pltpu.VMEM((half,) + slab, bf16),
             pltpu.VMEM((level_count,) + slab, bf16),
             *[pltpu.VMEM(shape, dtype) for shape, dtype in near],
-            dma((own, lat_size, lon_size)), dma((own, lat_size, lon_size)), dma((own,)), dma((10,)),
-            dma((lat_size,)), dma((lat_size,)), dma((half,)), dma((lon_size,)),
+            dma((own, lat_size, lon_size)), dma((own, lat_size, lon_size)), dma((own,)), dma((9,)),
+            dma((lat_size,)), dma((lat_size,)), dma((lat_size,)), dma((lat_size,)), dma((half,)), dma((lon_size,)),
             dma((lat_size,)), dma((lat_size,)), dma((lat_size,)), dma((lat_size,)),
-            dma((half,)), dma((half,)), dma((half, lat_size)), dma((half, lat_size)),
+            dma((half, lat_size // 2)), dma((half, lat_size // 2)), dma((half, lat_size)), dma((half, lat_size)),
             dma((half,)), dma((lon_size,)), dma((lon_size,)), dma((lon_size,)),
         ],
         compiler_params=pltpu.CompilerParams(

time: 137 us -> 132 us (0.964)
  Pallas kernels: 134 us -> 130 us
    pallas_call x1, Pallas kernels: 134 us -> 130 us  [local(): pl.pallas_call(functools.partial(fused_kernel, lat_size, lon_size, own, o...]
where the time goes in v2:
time: 132 us
  Pallas kernels  130 us (98%)
  other arithmetic  1.91 us (1%)
    pallas_call x1, Pallas kernels, local(): pl.pallas_call(functools.partial(fused_kernel, lat_size, lon_size, own, o...  130 us

profile of v2, /device:TPU:0, one launch (start us, length us, event | category | flops | bytes accessed | tf_op | source)
XLA Modules:
  0.0 132.2 jit_solution(14950568107982935508)
XLA Ops:
  0.0 130.2 %shard_map.100 = bf16[4,360,128]{2,1,0:T(8,128)(2,1)} custom-call(bf16[12,4,360,128]{3,2,1,0:T(8,128)(2,1)} %anom.1, f32[1,360,512]{2,1,0:T(8,128)} %taper.1, s32[64,128]{1,0:T(8,128)} %level.1, s32[64,128]{1,0:T(8,128)} %column.1, s32[64,128]{1,0:T(8,128)} %row.1, f32[64,128]{1,0:T(8,128)} %value.1, f32[2,2,15,1536]{3,2,1,0:T(8,128)} %constant.11.clone.lon_high, ...), custom_call_target="tpu_custom_call" | custom-call | tf_op jit(solution)/shard_map/pallas_call | solution.py:504
  130.3 1.9 %convert_multiply_fusion = f32[4,360,128]{2,1,0:T(8,128)} fusion(bf16[4,360,128]{2,1,0:T(8,128)(2,1)} %shard_map.100), kind=kLoop, calls=%fused_computation | loop fusion | flops 368640 | bytes 1105920 | tf_op jit(solution)/shard_map/div | solution.py:546

commit v3 on v2

--- a/solution.py
+++ b/solution.py
@@ -68,10 +68,10 @@
     lat_size, lon_size, own, obs_rows,
     anom, taper, level, column, row, value, lon_high, lon_low, lat_high, lat_low, out,
     fields, even_fwd, odd_fwd, even_inv, odd_inv, fine, modes, taper_near, taper_all, hits, innov_own, innov_all,
-    folded, zonal, spectrum, tapered, inverse, total, partner_part, lat_send, lat_recv, lon_send, lon_recv,
+    folded, zonal, spectrum, tapered, inverse, total, partner_part, lat_send, lat_recv, near_send, near_recv, lon_send, lon_recv,
     level_near, column_near, row_near, value_near, high_near, low_near, lat_high_near, lat_low_near,
     field_ss, field_rs, local_sem, table_sem, taper_ss, taper_rs, trade_ss, trade_rs, innov_ss, innov_rs,
-    gather_ss, gather_rs, share_ss, share_rs, mem_ss, mem_rs, lat_ss, lat_rs, lon_ss, lon_rs, pair_ss, pair_rs,
+    gather_ss, gather_rs, share_ss, share_rs, mem_ss, mem_rs, lat_ss, lat_rs, near_ss, near_rs, lon_ss, lon_rs, pair_ss, pair_rs, out_sem,
 ):
     lat, lon, mem = lax.axis_index("lat"), lax.axis_index("lon"), lax.axis_index("mem")
     place_count = lat_size * lon_size
@@ -119,8 +119,9 @@
         )
 
     def send_fields(turn, slot):
-        @pl.loop(1 if slot == 0 else 0, lon_size)
-        def _(step):
+        @pl.loop(0, lon_size - 1 if slot == 0 else lon_size)
+        def _(idx):
+            step = half + lax.div(idx + 1, 2) * (1 - 2 * lax.rem(idx, 2))
             field_copy(turn, slot, step).start()
 
     def own_copy(turn):
@@ -267,6 +268,8 @@
     def share_copy(slot):
         return remote(innov_all.at[slot], innov_all.at[slot], share_ss.at[slot], share_rs.at[slot], partner)
 
+    send_fields(1, 0)
+
     @pl.when(receives)
     def _():
         for step in range(1, lon_size):
@@ -280,7 +283,7 @@
         share_copy(0).start()
 
     for turn in range(1, own):
-        for slot in range(lat_size):
+        for slot in range(1 if turn == 1 else 0, lat_size):
             send_fields(turn, slot)
 
     @pl.when(receives)
@@ -319,49 +322,40 @@
         for idx, value in enumerate([even + odd, even - odd, first - third, second - last]):
             folded[pl.ds(idx * points, span), lanes] = value.astype(bf16)
 
+    def zonal_of(turn, stage):
+        for which in range(2):
+            slot = 2 * stage + which
+
+            @pl.loop(0, lon_size)
+            def _(step, slot=slot):
+                pl.when(slot + step == 0)(lambda: own_copy(turn).wait())
+                pl.when(slot + step > 0)(lambda: field_copy(turn, slot, step).wait_recv())
+
+            fold(turn, slot, slice(which * row_count, (which + 1) * row_count))
+        for kind in range(2):
+            zonal[kind * kind_size:(kind + 1) * kind_size, :] = jnp.dot(
+                even_fwd[kind], folded[kind * points:(kind + 1) * points, :], preferred_element_type=f32
+            ).astype(bf16)
+        zonal[2 * kind_size:, :] = jnp.dot(
+            odd_fwd[...], folded[2 * points:, :], preferred_element_type=f32
+        ).astype(bf16)
+        return jnp.dot(zonal[...], modes[stage * pair:(stage + 1) * pair, :], preferred_element_type=f32)
+
     def transform(turn):
-        @pl.loop(0, stages)
-        def _(stage):
-            for which in range(2):
-                slot = 2 * stage + which
-
-                @pl.loop(0, lon_size)
-                def _(step, slot=slot):
-                    pl.when(slot + step == 0)(lambda: own_copy(turn).wait())
-                    pl.when(slot + step > 0)(lambda: field_copy(turn, slot, step).wait_recv())
-
-                fold(turn, slot, slice(which * row_count, (which + 1) * row_count))
-            for kind in range(2):
-                zonal[kind * kind_size:(kind + 1) * kind_size, :] = jnp.dot(
-                    even_fwd[kind], folded[kind * points:(kind + 1) * points, :], preferred_element_type=f32
-                ).astype(bf16)
-            zonal[2 * kind_size:, :] = jnp.dot(
-                odd_fwd[...], folded[2 * points:, :], preferred_element_type=f32
-            ).astype(bf16)
-            terms = jnp.dot(
-                zonal[...], modes[pl.ds(pl.multiple_of(stage * pair, pair), pair), :], preferred_element_type=f32
-            )
-
-            @pl.when(stage == 0)
-            def _():
-                spectrum[...] = terms
-
-            @pl.when(stage > 0)
-            def _():
-                spectrum[...] += terms
-
-        tapered[...] = (
-            spectrum[...] * taper_all[...].reshape(kinds, lat_size * row_count).astype(f32)
+        for stage in range(stages - 1):
+            terms = zonal_of(turn, stage)
+            spectrum[...] = terms if stage == 0 else spectrum[...] + terms
+        terms = zonal_of(turn, stages - 1) + spectrum[...]
+        tapered[...] = (terms * taper_all[...].reshape(kinds, lat_size * row_count).astype(f32)).astype(bf16)
+
+    def localize(turn, stage):
+        inverse[...] = lax.dot_general(
+            tapered[...], modes[pl.ds(pl.multiple_of(stage * pair, pair), pair), :],
+            (((1,), (1,)), ((), ())), preferred_element_type=f32,
         ).astype(bf16)
-        inverse[...] = lax.dot_general(
-            tapered[...], modes[...], (((1,), (1,)), ((), ())), preferred_element_type=f32
-        ).astype(bf16)
-
-    def localize(turn, stage):
-        lanes = pl.ds(pl.multiple_of(stage * pair, pair), pair)
 
         def back(table, rows):
-            return jnp.dot(table, inverse[rows, lanes], preferred_element_type=f32)
+            return jnp.dot(table, inverse[rows, :], preferred_element_type=f32)
 
         even = back(even_inv[0, :span], slice(0, kind_size))
         swing = back(even_inv[1, :span], slice(kind_size, 2 * kind_size))
@@ -399,78 +393,133 @@
         for idx in range(half):
             mem_copy(idx, stage).start()
 
-    def lat_copy(idx, slot):
-        return remote(
-            lat_send.at[idx, slot], lat_recv.at[idx, slot], lat_ss.at[idx, slot], lat_rs.at[idx, slot],
+    cutoff = col_count // 2 // 16 * 16
+    bands = [slice(0, cutoff), slice(cutoff, col_count)]
+
+    def lat_copy(idx, slot, band):
+        rows = bands[band]
+        return remote(
+            lat_send.at[idx, slot, rows], lat_recv.at[idx, slot, rows],
+            lat_ss.at[idx, slot, band], lat_rs.at[idx, slot, band],
             device(lax.rem(lat + lat_size - slot, lat_size), lon, mem),
         )
 
-    @pl.loop(0, half)
-    def _(idx):
+    def near_copy(idx, slot):
+        return remote(
+            near_send.at[idx, slot], near_recv.at[lax.rem(lon, half), slot],
+            near_ss.at[idx, slot], near_rs.at[lax.rem(lon, half), slot],
+            device(lax.rem(lat + lat_size - slot, lat_size), owned(quarter + idx, mem), mem),
+        )
+
+    slots = range(lat_size - 1, -1, -1)
+    for idx in range(quarter):
         block = owned(idx, mem)
-        for stage in range(stages - 1, -1, -1):
-            mem_copy(idx, stage).wait_recv()
-            for slot in (2 * stage + 1, 2 * stage):
-                lat_send[idx, slot] = (total[block, slot] + partner_part[idx, slot]).astype(bf16)
+        for band in range(2):
+            for slot in slots:
+                if band == 0 and slot % 2 == 1:
+                    mem_copy(idx, slot // 2).wait_recv()
+                rows = bands[band]
+                lat_send[idx, slot, rows] = (total[block, slot, rows] + partner_part[idx, slot, rows]).astype(bf16)
                 if slot > 0:
-                    lat_copy(idx, slot).start()
-
-    def lon_copy(idx):
-        return remote(
-            lon_send.at[idx], lon_recv.at[lon], lon_ss.at[idx], lon_rs.at[lon], device(lat, owned(idx, mem), mem)
-        )
-
-    for idx in range(half):
-        summed = lat_send[idx, 0].astype(f32)
-        for slot in range(1, lat_size):
-            lat_copy(idx, slot).wait_recv()
-            summed += lat_recv[idx, slot].astype(f32)
-        block = owned(idx, mem)
-        lon_send[idx] = summed.astype(bf16)
-        pl.when(block != lon)(lambda idx=idx: lon_copy(idx).start())
-
-        @pl.when(block == lon)
-        def _(idx=idx):
-            lon_recv[lon] = lon_send[idx]
+                    lat_copy(idx, slot, band).start()
+    for idx in range(quarter):
+        block = owned(quarter + idx, mem)
+        for slot in slots:
+            if slot % 2 == 1:
+                mem_copy(quarter + idx, slot // 2).wait_recv()
+            value = (total[block, slot] + partner_part[quarter + idx, slot]).astype(bf16)
+            if slot > 0:
+                near_send[idx, slot] = value
+                near_copy(idx, slot).start()
+            else:
+                @pl.when(block != lon)
+                def _(idx=idx, value=value):
+                    near_send[idx, 0] = value
+                    near_copy(idx, 0).start()
+
+                @pl.when(block == lon)
+                def _(value=value):
+                    near_recv[lax.rem(lon, half), 0] = value
+
+    def lon_copy(idx, band):
+        rows = bands[band]
+        return remote(
+            lon_send.at[idx, rows], lon_recv.at[lon, rows], lon_ss.at[idx, band], lon_rs.at[lon, band],
+            device(lat, owned(idx, mem), mem),
+        )
+
+    for band in range(2):
+        rows = bands[band]
+        for idx in range(quarter):
+            summed = lat_send[idx, 0, rows].astype(f32)
+            for slot in range(1, lat_size):
+                lat_copy(idx, slot, band).wait_recv()
+                summed += lat_recv[idx, slot, rows].astype(f32)
+            lon_send[idx, rows] = summed.astype(bf16)
+            lon_copy(idx, band).start()
 
     def pair_copy(sender):
-        return remote(lon_recv.at[sender], lon_recv.at[sender], pair_ss.at[sender], pair_rs.at[sender], partner)
+        return remote(lon_recv.at[sender], out.at[sender], pair_ss.at[sender], pair_rs.at[sender], partner)
+
+    def out_copy(sender):
+        return pltpu.make_async_copy(lon_recv.at[sender], out.at[sender], out_sem.at[sender])
 
     far = [(1 - side) * half + idx for idx in range(half)]
-    close = [side * half + lax.rem(lon + idx, half) for idx in range(1, half)]
+    close = [side * half + lax.rem(lon + idx, half) for idx in range(half)]
 
     @pl.when(receives)
     def _():
-        pair_copy(lon).start()
-        for sender in far + close:
-            remote(
-                lon_send.at[0], lon_recv.at[sender], lon_ss.at[0], lon_rs.at[sender], device(lat, sender, mem)
-            ).wait_recv()
+        for idx, sender in enumerate(close):
+            local_level = lax.rem(lon + idx, half)
+            summed = None
+            for slot in range(lat_size):
+                if idx + slot > 0:
+                    remote(
+                        near_send.at[0, slot], near_recv.at[local_level, slot], near_ss.at[0, slot],
+                        near_rs.at[local_level, slot], device(lax.rem(lat + slot, lat_size), sender, mem),
+                    ).wait_recv()
+                term = near_recv[local_level, slot].astype(f32)
+                summed = term if slot == 0 else summed + term
+            lon_recv[sender] = summed.astype(bf16)
             pair_copy(sender).start()
+            out_copy(sender).start()
+        for sender in far:
+            for band in range(2):
+                rows = bands[band]
+                remote(
+                    lon_send.at[0, rows], lon_recv.at[sender, rows], lon_ss.at[0, band], lon_rs.at[sender, band],
+                    device(lat, sender, mem),
+                ).wait_recv()
+            pair_copy(sender).start()
+            out_copy(sender).start()
 
     @pl.when(jnp.logical_not(receives))
     def _():
-        for sender in far + close + [lon]:
+        for sender in close + far:
             pair_copy(sender).wait_recv()
-
-    out[...] = lon_recv[...]
 
     @pl.when(receives)
     def _():
-        for sender in far + close + [lon]:
+        for sender in close + far:
             pair_copy(sender).wait_send()
+            out_copy(sender).wait()
         for slot in range(1, lat_size):
             gather_copy(slot).wait_send()
         for slot in range(lat_size):
             share_copy(slot).wait_send()
 
     for idx in range(half):
-        pl.when(owned(idx, mem) != lon)(lambda idx=idx: lon_copy(idx).wait_send())
         pl.when(owned(idx, mem) != lon)(lambda idx=idx: innov_copy(idx).wait_send())
         for stage in range(stages):
             mem_copy(idx, stage).wait_send()
+    for idx in range(quarter):
+        for band in range(2):
+            lon_copy(idx, band).wait_send()
+            for slot in range(1, lat_size):
+                lat_copy(idx, slot, band).wait_send()
         for slot in range(1, lat_size):
-            lat_copy(idx, slot).wait_send()
+            near_copy(idx, slot).wait_send()
+        pl.when(owned(quarter + idx, mem) != lon)(lambda idx=idx: near_copy(idx, 0).wait_send())
     for step in range(1, lat_size):
         taper_copy(step).wait_send()
         trade_copy(step).wait_send()
@@ -505,7 +554,7 @@
         functools.partial(fused_kernel, lat_size, lon_size, own, obs_row.shape[0]),
         out_shape=jax.ShapeDtypeStruct((level_count,) + slab, bf16),
         in_specs=[whole] * 10,
-        out_specs=pl.BlockSpec(memory_space=pltpu.VMEM),
+        out_specs=whole,
         scratch_shapes=[
             pltpu.VMEM((own, lat_size, lon_size) + slab, bf16),
             pltpu.VMEM((2, kind_size, points), bf16),
@@ -523,19 +572,22 @@
             pltpu.VMEM((4 * kind_size, 2 * row_count), bf16),
             pltpu.VMEM((4 * kind_size, lat_total), f32),
             pltpu.VMEM((4 * kind_size, lat_total), bf16),
-            pltpu.VMEM((4 * kind_size, lat_total), bf16),
+            pltpu.VMEM((4 * kind_size, 2 * row_count), bf16),
             pltpu.VMEM((lon_size, lat_size) + slab, f32),
             pltpu.VMEM((half, lat_size) + slab, f32),
+            pltpu.VMEM((half // 2, lat_size) + slab, bf16),
+            pltpu.VMEM((half // 2, lat_size) + slab, bf16),
+            pltpu.VMEM((half // 2, lat_size) + slab, bf16),
             pltpu.VMEM((half, lat_size) + slab, bf16),
-            pltpu.VMEM((half, lat_size) + slab, bf16),
-            pltpu.VMEM((half,) + slab, bf16),
+            pltpu.VMEM((half // 2,) + slab, bf16),
             pltpu.VMEM((level_count,) + slab, bf16),
             *[pltpu.VMEM(shape, dtype) for shape, dtype in near],
             dma((own, lat_size, lon_size)), dma((own, lat_size, lon_size)), dma((own,)), dma((9,)),
             dma((lat_size,)), dma((lat_size,)), dma((lat_size,)), dma((lat_size,)), dma((half,)), dma((lon_size,)),
             dma((lat_size,)), dma((lat_size,)), dma((lat_size,)), dma((lat_size,)),
-            dma((half, lat_size // 2)), dma((half, lat_size // 2)), dma((half, lat_size)), dma((half, lat_size)),
-            dma((half,)), dma((lon_size,)), dma((lon_size,)), dma((lon_size,)),
+            dma((half, lat_size // 2)), dma((half, lat_size // 2)), dma((half // 2, lat_size, 2)),
+            dma((half // 2, lat_size, 2)), dma((half // 2, lat_size)), dma((half, lat_size)),
+            dma((half // 2, 2)), dma((lon_size, 2)), dma((lon_size,)), dma((lon_size,)), dma((lon_size,)),
         ],
         compiler_params=pltpu.CompilerParams(
             collective_id=0, has_side_effects=True, vmem_limit_bytes=60 * 1024 * 1024

time: 132 us -> 131 us (level)
  Pallas kernels: 130 us -> 128 us
    pallas_call x1, Pallas kernels: 130 us -> 128 us  [local(): pl.pallas_call(functools.partial(fused_kernel, lat_size, lon_size, own, o...]
where the time goes in v3:
time: 131 us; the launch traced here: 130 us
  Pallas kernels  128 us (98%)
  other arithmetic  1.91 us (1%)
    pallas_call x1, Pallas kernels, local(): pl.pallas_call(functools.partial(fused_kernel, lat_size, lon_size, own, o...  128 us

profile of v3, /device:TPU:0, one launch (start us, length us, event | category | flops | bytes accessed | tf_op | source)
XLA Modules:
  0.0 130.4 jit_solution(14506389624339732999)
XLA Ops:
  0.0 128.5 %shard_map.100 = bf16[4,360,128]{2,1,0:T(8,128)(2,1)} custom-call(bf16[12,4,360,128]{3,2,1,0:T(8,128)(2,1)} %anom.1, f32[1,360,512]{2,1,0:T(8,128)} %taper.1, s32[64,128]{1,0:T(8,128)} %level.1, s32[64,128]{1,0:T(8,128)} %column.1, s32[64,128]{1,0:T(8,128)} %row.1, f32[64,128]{1,0:T(8,128)} %value.1, f32[2,2,15,1536]{3,2,1,0:T(8,128)} %constant.11.clone.lon_high, ...), custom_call_target="tpu_custom_call" | custom-call | tf_op jit(solution)/shard_map/pallas_call | solution.py:553
  128.5 1.9 %convert_multiply_fusion = f32[4,360,128]{2,1,0:T(8,128)} fusion(bf16[4,360,128]{2,1,0:T(8,128)(2,1)} %shard_map.100), kind=kLoop, calls=%fused_computation | loop fusion | flops 368640 | bytes 1105920 | tf_op jit(solution)/shard_map/div | solution.py:598

commit v4 on v3

--- a/solution.py
+++ b/solution.py
@@ -67,10 +67,10 @@
 def fused_kernel(
     lat_size, lon_size, own, obs_rows,
     anom, taper, level, column, row, value, lon_high, lon_low, lat_high, lat_low, out,
-    fields, even_fwd, odd_fwd, even_inv, odd_inv, fine, modes, taper_near, taper_all, hits, innov_own, innov_all,
+    fields, even_fwd, odd_fwd, even_inv, odd_inv, fine, modes, taper_near, taper_all, far_send, far_recv, far_near, far_hits, hits, innov_own, innov_all,
     folded, zonal, spectrum, tapered, inverse, total, partner_part, lat_send, lat_recv, near_send, near_recv, lon_send, lon_recv,
     level_near, column_near, row_near, value_near, high_near, low_near, lat_high_near, lat_low_near,
-    field_ss, field_rs, local_sem, table_sem, taper_ss, taper_rs, trade_ss, trade_rs, innov_ss, innov_rs,
+    field_ss, field_rs, local_sem, table_sem, taper_ss, taper_rs, trade_ss, trade_rs, far_ss, far_rs, innov_ss, innov_rs,
     gather_ss, gather_rs, share_ss, share_rs, mem_ss, mem_rs, lat_ss, lat_rs, near_ss, near_rs, lon_ss, lon_rs, pair_ss, pair_rs, out_sem,
 ):
     lat, lon, mem = lax.axis_index("lat"), lax.axis_index("lon"), lax.axis_index("mem")
@@ -98,40 +98,6 @@
         near = lax.div(idx, quarter)
         return (1 - side + near * (2 * side - 1)) * half + core * quarter + lax.rem(idx, quarter)
 
-    barrier = pltpu.get_barrier_semaphore()
-
-    @pl.loop(1, place_count)
-    def _(offset):
-        spot = lax.rem(me + offset, place_count)
-        pl.semaphore_signal(
-            barrier, inc=1, device_id=device(lax.div(spot, lon_size), lax.rem(spot, lon_size), mem),
-            device_id_type=pl.DeviceIdType.MESH,
-        )
-
-    pl.semaphore_signal(barrier, inc=1, device_id=partner, device_id_type=pl.DeviceIdType.MESH)
-    pl.semaphore_wait(barrier, place_count)
-
-    def field_copy(turn, slot, step):
-        lat_idx, lon_idx = lax.rem(lat + slot, lat_size), lax.rem(lon + step, lon_size)
-        return remote(
-            anom.at[lat_idx * own + turn, lon_idx], fields.at[turn, slot, lon],
-            field_ss.at[turn, slot, step], field_rs.at[turn, slot, step], device(lat_idx, lon_idx, mem),
-        )
-
-    def send_fields(turn, slot):
-        @pl.loop(0, lon_size - 1 if slot == 0 else lon_size)
-        def _(idx):
-            step = half + lax.div(idx + 1, 2) * (1 - 2 * lax.rem(idx, 2))
-            field_copy(turn, slot, step).start()
-
-    def own_copy(turn):
-        return pltpu.make_async_copy(
-            anom.at[lat * own + turn, lon], fields.at[turn, 0, lon], local_sem.at[turn]
-        )
-
-    lead = lat_size // 2
-    for slot in range(lead):
-        send_fields(0, slot)
     near_copies = [
         pltpu.make_async_copy(src, dst, table_sem.at[idx])
         for idx, (src, dst) in enumerate([
@@ -142,14 +108,66 @@
     ]
     for copy in near_copies:
         copy.start()
+    col_start, row_start = lon * col_count, lat * row_count
+    for copy in near_copies[:4]:
+        copy.wait()
+
+    local_col = column_near[...] - col_start
+    pairs = lax.shift_right_logical(local_col, 1).astype(f32).astype(bf16)
+    parities = (2 * (row_near[...] - row_start) + lax.bitwise_and(local_col, 1)).astype(f32).astype(bf16)
+    for idx in range(quarter):
+        far_send[idx, 0] = jnp.where(level_near[...] == owned(idx, mem), value_near[...], 0.0).astype(bf16)
+        far_send[idx, 1] = pairs
+        far_send[idx, 2] = parities
+
+    barrier = pltpu.get_barrier_semaphore()
+
+    @pl.loop(1, place_count)
+    def _(offset):
+        spot = lax.rem(me + offset, place_count)
+        pl.semaphore_signal(
+            barrier, inc=1, device_id=device(lax.div(spot, lon_size), lax.rem(spot, lon_size), mem),
+            device_id_type=pl.DeviceIdType.MESH,
+        )
+
+    pl.semaphore_signal(barrier, inc=1, device_id=partner, device_id_type=pl.DeviceIdType.MESH)
+    pl.semaphore_wait(barrier, place_count)
+
+    def far_copy(idx):
+        return remote(
+            far_send.at[idx], far_recv.at[lax.rem(lon, half)], far_ss.at[idx], far_rs.at[lax.rem(lon, half)],
+            device(lat, owned(idx, mem), mem),
+        )
+
+    for idx in range(quarter):
+        far_copy(idx).start()
+
+    def field_copy(turn, slot, step):
+        lat_idx, lon_idx = lax.rem(lat + slot, lat_size), lax.rem(lon + step, lon_size)
+        return remote(
+            anom.at[lat_idx * own + turn, lon_idx], fields.at[turn, slot, lon],
+            field_ss.at[turn, slot, step], field_rs.at[turn, slot, step], device(lat_idx, lon_idx, mem),
+        )
+
+    def send_fields(turn, slot):
+        @pl.loop(0, lon_size - 1 if slot == 0 else lon_size)
+        def _(idx):
+            step = half + lax.div(idx + 1, 2) * (1 - 2 * lax.rem(idx, 2))
+            field_copy(turn, slot, step).start()
+
+    def own_copy(turn):
+        return pltpu.make_async_copy(
+            anom.at[lat * own + turn, lon], fields.at[turn, 0, lon], local_sem.at[turn]
+        )
+
+    lead = lat_size // 2
+    for slot in range(lead):
+        send_fields(0, slot)
     for turn in range(own):
         own_copy(turn).start()
 
     hits[...] = jnp.zeros_like(hits)
-    col_start, row_start = lon * col_count, lat * row_count
     group = 4
-    for copy in near_copies[:4]:
-        copy.wait()
 
     @pl.loop(0, obs_rows // group)
     def _(step):
@@ -167,22 +185,22 @@
             [jnp.where(row_hot, high, 0.0).astype(bf16), jnp.where(row_hot, low, 0.0).astype(bf16)], axis=0
         )
         cells = lax.broadcasted_iota(jnp.int32, (col_count, width), 0)
-        for idx in range(half):
-            left = jnp.where(cells == keys - owned(idx, mem) * col_count, 1.0, 0.0).astype(bf16)
+        for idx in range(quarter):
+            left = jnp.where(cells == keys - owned(quarter + idx, mem) * col_count, 1.0, 0.0).astype(bf16)
             hits[idx] += lax.dot_general(
                 left, right, (((1,), (1,)), ((), ())), preferred_element_type=f32
             )
 
     def innov_copy(idx):
-        lev = owned(idx, mem)
+        lev = owned(quarter + idx, mem)
         return remote(
             innov_own.at[idx], innov_all.at[0, lon], innov_ss.at[idx], innov_rs.at[lon], device(lat, lev, mem)
         )
 
-    for idx in range(half):
+    for idx in range(quarter):
         block = (hits[idx, :, :row_count] + hits[idx, :, row_count:]).astype(bf16)
         innov_own[idx] = block
-        lev = owned(idx, mem)
+        lev = owned(quarter + idx, mem)
         pl.when(lev != lon)(lambda idx=idx: innov_copy(idx).start())
 
         @pl.when(lev == lon)
@@ -191,6 +209,57 @@
 
     for slot in range(lead, lat_size):
         send_fields(0, slot)
+    def gather_copy(slot):
+        return remote(
+            innov_all.at[0], innov_all.at[slot], gather_ss.at[slot], gather_rs.at[slot],
+            device(lax.rem(lat + slot, lat_size), lon, mem),
+        )
+
+    def share_copy(slot):
+        return remote(innov_all.at[slot], innov_all.at[slot], share_ss.at[slot], share_rs.at[slot], partner)
+
+    @pl.when(receives)
+    def _():
+        @pl.loop(0, half)
+        def _(source):
+            remote(
+                far_send.at[0], far_recv.at[source], far_ss.at[0], far_rs.at[source],
+                device(lat, (1 - side) * half + source, mem),
+            ).wait_recv()
+            far_near[...] = far_recv[source].astype(f32)
+            far_hits[...] = jnp.zeros_like(far_hits)
+
+            @pl.loop(0, obs_rows // group)
+            def _(step):
+                def wide(kind):
+                    return jnp.concatenate(
+                        [far_near[kind, pl.ds(step * group + part, 1), :] for part in range(group)], axis=1
+                    )
+
+                coded = wide(2).astype(jnp.int32)
+                local_row = lax.shift_right_logical(coded, 1)
+                local_col = 2 * wide(1).astype(jnp.int32) + lax.bitwise_and(coded, 1)
+                width = coded.shape[1]
+                row_hot = lax.broadcasted_iota(jnp.int32, (row_count, width), 0) == local_row
+                right = jnp.where(row_hot, wide(0), 0.0).astype(bf16)
+                cells = lax.broadcasted_iota(jnp.int32, (col_count, width), 0)
+                left = jnp.where(cells == local_col, 1.0, 0.0).astype(bf16)
+                far_hits[...] += lax.dot_general(
+                    left, right, (((1,), (1,)), ((), ())), preferred_element_type=f32
+                )
+
+            innov_all[0, (1 - side) * half + source] = far_hits[...].astype(bf16)
+
+        for idx in range(1, half):
+            sender = side * half + lax.rem(lon + idx, half)
+            remote(
+                innov_own.at[0], innov_all.at[0, sender], innov_ss.at[0], innov_rs.at[sender],
+                device(lat, sender, mem),
+            ).wait_recv()
+        for slot in range(1, lat_size):
+            gather_copy(slot).start()
+        share_copy(0).start()
+
     near_copies[4].wait()
     share, share_pad = taper_near.shape[0] // 4, taper_all.shape[2]
     modes_half = taper_near.shape[1] // 2
@@ -220,6 +289,11 @@
 
     for step in range(1, lat_size):
         taper_copy(step).start()
+
+    for turn in range(1, own):
+        for slot in range(lat_size):
+            send_fields(turn, slot)
+
     for copy in near_copies[5:]:
         copy.wait()
 
@@ -258,33 +332,6 @@
             modes[rows, :] = (
                 lat_high_near[0, spot, :] * lat_cos - lat_high_near[1, spot, :] * lat_sin
             ).astype(bf16)
-
-    def gather_copy(slot):
-        return remote(
-            innov_all.at[0], innov_all.at[slot], gather_ss.at[slot], gather_rs.at[slot],
-            device(lax.rem(lat + slot, lat_size), lon, mem),
-        )
-
-    def share_copy(slot):
-        return remote(innov_all.at[slot], innov_all.at[slot], share_ss.at[slot], share_rs.at[slot], partner)
-
-    send_fields(1, 0)
-
-    @pl.when(receives)
-    def _():
-        for step in range(1, lon_size):
-            sender = lax.rem(lon + step, lon_size)
-            remote(
-                innov_own.at[0], innov_all.at[0, sender], innov_ss.at[0], innov_rs.at[sender],
-                device(lat, sender, mem),
-            ).wait_recv()
-        for slot in range(1, lat_size):
-            gather_copy(slot).start()
-        share_copy(0).start()
-
-    for turn in range(1, own):
-        for slot in range(1 if turn == 1 else 0, lat_size):
-            send_fields(turn, slot)
 
     @pl.when(receives)
     def _():
@@ -509,7 +556,6 @@
             share_copy(slot).wait_send()
 
     for idx in range(half):
-        pl.when(owned(idx, mem) != lon)(lambda idx=idx: innov_copy(idx).wait_send())
         for stage in range(stages):
             mem_copy(idx, stage).wait_send()
     for idx in range(quarter):
@@ -520,6 +566,8 @@
         for slot in range(1, lat_size):
             near_copy(idx, slot).wait_send()
         pl.when(owned(quarter + idx, mem) != lon)(lambda idx=idx: near_copy(idx, 0).wait_send())
+        pl.when(owned(quarter + idx, mem) != lon)(lambda idx=idx: innov_copy(idx).wait_send())
+        far_copy(idx).wait_send()
     for step in range(1, lat_size):
         taper_copy(step).wait_send()
         trade_copy(step).wait_send()
@@ -565,8 +613,12 @@
             pltpu.VMEM((lat_total, lat_total), bf16),
             pltpu.VMEM((part_count, lat_total), f32),
             pltpu.VMEM((4, lat_size, share_pad, lat_total), bf16),
-            pltpu.VMEM((half, col_count, 2 * row_count), f32),
-            pltpu.VMEM((half,) + slab, bf16),
+            pltpu.VMEM((half // 2, 3) + obs_row.shape, bf16),
+            pltpu.VMEM((half, 3) + obs_row.shape, bf16),
+            pltpu.VMEM((3,) + obs_row.shape, f32),
+            pltpu.VMEM(slab, f32),
+            pltpu.VMEM((half // 2, col_count, 2 * row_count), f32),
+            pltpu.VMEM((half // 2,) + slab, bf16),
             pltpu.VMEM((lat_size, lon_size) + slab, bf16),
             pltpu.VMEM((4 * points, 2 * row_count), bf16),
             pltpu.VMEM((4 * kind_size, 2 * row_count), bf16),
@@ -583,7 +635,8 @@
             pltpu.VMEM((level_count,) + slab, bf16),
             *[pltpu.VMEM(shape, dtype) for shape, dtype in near],
             dma((own, lat_size, lon_size)), dma((own, lat_size, lon_size)), dma((own,)), dma((9,)),
-            dma((lat_size,)), dma((lat_size,)), dma((lat_size,)), dma((lat_size,)), dma((half,)), dma((lon_size,)),
+            dma((lat_size,)), dma((lat_size,)), dma((lat_size,)), dma((lat_size,)),
+            dma((half // 2,)), dma((half,)), dma((half // 2,)), dma((lon_size,)),
             dma((lat_size,)), dma((lat_size,)), dma((lat_size,)), dma((lat_size,)),
             dma((half, lat_size // 2)), dma((half, lat_size // 2)), dma((half // 2, lat_size, 2)),
             dma((half // 2, lat_size, 2)), dma((half // 2, lat_size)), dma((half, lat_size)),

time: 131 us -> 129 us (0.985)
    pallas_call x1, Pallas kernels: 128 us -> 127 us  [local(): pl.pallas_call(functools.partial(fused_kernel, lat_size, lon_size, own, o...]
where the time goes in v4:
time: 129 us
  Pallas kernels  127 us (98%)
  other arithmetic  1.91 us (1%)
    pallas_call x1, Pallas kernels, local(): pl.pallas_call(functools.partial(fused_kernel, lat_size, lon_size, own, o...  127 us

profile of v4, /device:TPU:0, one launch (start us, length us, event | category | flops | bytes accessed | tf_op | source)
XLA Modules:
  0.0 129.0 jit_solution(15075735431706192068)
XLA Ops:
  0.0 127.1 %shard_map.100 = bf16[4,360,128]{2,1,0:T(8,128)(2,1)} custom-call(bf16[12,4,360,128]{3,2,1,0:T(8,128)(2,1)} %anom.1, f32[1,360,512]{2,1,0:T(8,128)} %taper.1, s32[64,128]{1,0:T(8,128)} %level.1, s32[64,128]{1,0:T(8,128)} %column.1, s32[64,128]{1,0:T(8,128)} %row.1, f32[64,128]{1,0:T(8,128)} %value.1, f32[2,2,15,1536]{3,2,1,0:T(8,128)} %constant.11.clone.lon_high, ...), custom_call_target="tpu_custom_call" | custom-call | tf_op jit(solution)/shard_map/pallas_call | solution.py:601
  127.1 1.9 %convert_multiply_fusion = f32[4,360,128]{2,1,0:T(8,128)} fusion(bf16[4,360,128]{2,1,0:T(8,128)(2,1)} %shard_map.100), kind=kLoop, calls=%fused_computation | loop fusion | flops 368640 | bytes 1105920 | tf_op jit(solution)/shard_map/div | solution.py:651

commit v5 on v4

--- a/solution.py
+++ b/solution.py
@@ -290,9 +290,15 @@
     for step in range(1, lat_size):
         taper_copy(step).start()
 
-    for turn in range(1, own):
+    for turn in range(1, own - 1):
         for slot in range(lat_size):
             send_fields(turn, slot)
+
+    @pl.loop(0, lon_size)
+    def _(idx):
+        step = half + lax.div(idx + 1, 2) * (1 - 2 * lax.rem(idx, 2))
+        for slot in range(lat_size):
+            pl.when(slot + step > 0)(lambda slot=slot: field_copy(own - 1, slot, step).start())
 
     for copy in near_copies[5:]:
         copy.wait()

time: 129 us -> 126 us (0.977)
  Pallas kernels: 127 us -> 124 us
    pallas_call x1, Pallas kernels: 127 us -> 124 us  [local(): pl.pallas_call(functools.partial(fused_kernel, lat_size, lon_size, own, o...]
where the time goes in v5:
time: 126 us
  Pallas kernels  124 us (98%)
  other arithmetic  1.91 us (2%)
    pallas_call x1, Pallas kernels, local(): pl.pallas_call(functools.partial(fused_kernel, lat_size, lon_size, own, o...  124 us

profile of v5, /device:TPU:0, one launch (start us, length us, event | category | flops | bytes accessed | tf_op | source)
XLA Modules:
  0.0 126.3 jit_solution(6552388611824028116)
XLA Ops:
  0.0 124.4 %shard_map.100 = bf16[4,360,128]{2,1,0:T(8,128)(2,1)} custom-call(bf16[12,4,360,128]{3,2,1,0:T(8,128)(2,1)} %anom.1, f32[1,360,512]{2,1,0:T(8,128)} %taper.1, s32[64,128]{1,0:T(8,128)} %level.1, s32[64,128]{1,0:T(8,128)} %column.1, s32[64,128]{1,0:T(8,128)} %row.1, f32[64,128]{1,0:T(8,128)} %value.1, f32[2,2,15,1536]{3,2,1,0:T(8,128)} %constant.11.clone.lon_high, ...), custom_call_target="tpu_custom_call" | custom-call | tf_op jit(solution)/shard_map/pallas_call | solution.py:607
  124.4 1.9 %convert_multiply_fusion = f32[4,360,128]{2,1,0:T(8,128)} fusion(bf16[4,360,128]{2,1,0:T(8,128)(2,1)} %shard_map.100), kind=kLoop, calls=%fused_computation | loop fusion | flops 368640 | bytes 1105920 | tf_op jit(solution)/shard_map/div | solution.py:657

commit v6 on v5

--- a/solution.py
+++ b/solution.py
@@ -439,9 +439,7 @@
             mem_ss.at[idx, stage], mem_rs.at[idx, stage], partner,
         )
 
-    @pl.loop(0, stages)
-    def _(step):
-        stage = stages - 1 - step
+    for stage in range(stages - 1, -1, -1):
         localize(own - 1, stage)
         for idx in range(half):
             mem_copy(idx, stage).start()

time: 126 us -> 125 us (level)
  no operation moved by 1% of the time
where the time goes in v6:
time: 125 us
  Pallas kernels  123 us (98%)
  other arithmetic  1.91 us (2%)
    pallas_call x1, Pallas kernels, local(): pl.pallas_call(functools.partial(fused_kernel, lat_size, lon_size, own, o...  123 us

profile of v6, /device:TPU:0, one launch (start us, length us, event | category | flops | bytes accessed | tf_op | source)
XLA Modules:
  0.0 125.2 jit_solution(8969802287531288574)
XLA Ops:
  0.0 123.3 %shard_map.100 = bf16[4,360,128]{2,1,0:T(8,128)(2,1)} custom-call(bf16[12,4,360,128]{3,2,1,0:T(8,128)(2,1)} %anom.1, f32[1,360,512]{2,1,0:T(8,128)} %taper.1, s32[64,128]{1,0:T(8,128)} %level.1, s32[64,128]{1,0:T(8,128)} %column.1, s32[64,128]{1,0:T(8,128)} %row.1, f32[64,128]{1,0:T(8,128)} %value.1, f32[2,2,15,1536]{3,2,1,0:T(8,128)} %constant.11.clone.lon_high, ...), custom_call_target="tpu_custom_call" | custom-call | tf_op jit(solution)/shard_map/pallas_call | solution.py:605
  123.3 1.9 %convert_multiply_fusion = f32[4,360,128]{2,1,0:T(8,128)} fusion(bf16[4,360,128]{2,1,0:T(8,128)(2,1)} %shard_map.100), kind=kLoop, calls=%fused_computation | loop fusion | flops 368640 | bytes 1105920 | tf_op jit(solution)/shard_map/div | solution.py:655
